TPU v7x, 128 devices: a whole 4x4x4 slice. The times are simulated.
128 devices in a mesh: row: 8 (over x, y_lo), col: 16 (over y_hi, z, core).
Axes of the slice: x: 4, y: 4 (y_hi: 2, y_lo: 2; y = y_hi * 2 + y_lo), z: 4, core: 2. Of those that a mesh axis runs over, the one named last changes fastest.
Arguments:
- tokens: bfloat16 [1024, 5120], P('row'), may hold values from -6 to 6
- expert_ids: int32 [1024], replicated, may hold values from 0 to 15
- modality: int32 [1024], replicated, may hold values from 0 to 1
- tile_counts: int32 [2, 16], replicated, may hold values from 1 to 4, as said below
- router: bfloat16 [5120, 16], P(None, 'col'), may hold values from -0.15625 to 0.15625
- w_gate: bfloat16 [16, 5120, 4096], P('col', None, 'row'), may hold values from -0.078125 to 0.078125
- w_up: bfloat16 [16, 5120, 4096], P('col', None, 'row'), may hold values from -0.078125 to 0.078125
- w_down: bfloat16 [16, 4096, 5120], P('col', 'row'), may hold values from -0.09375 to 0.09375
- shared_gate: bfloat16 [5120, 8192], P('row', 'col'), may hold values from -0.078125 to 0.078125
- shared_up: bfloat16 [5120, 8192], P('row', 'col'), may hold values from -0.078125 to 0.078125
- shared_down: bfloat16 [8192, 5120], P('col', 'row'), may hold values from -0.0625 to 0.0625
Outputs:
- mixed: bfloat16 [1024, 5120], P('col', 'row')
Inputs may be any that keep to these rules, and one draw needn't show every extreme that they name: `tile_counts`: in every draw some expert's text segment has 4 tiles and at least 32 text tokens, and some expert's image segment has 4 tiles and at least 32 image tokens.
All inputs are finite; a program needn't handle non-finite values.
Results may differ from a plain program's by a relative error of at most 0.0052.
Values may be sent and summed in bfloat16 or wider, within the bound.
A program may use at most 128 MiB of HBM per device.

v0:
```python
import jax
import jax.numpy as jnp
from jax import lax
from jax.sharding import Mesh
from jax.sharding import PartitionSpec as P

TILE = 8
MAXT = 4
ROW = ("row_0", "row_1")


def whole_of(array, axes, dim):
    whole = array
    for number in range(len(axes) - 1, -1, -1):
        whole = lax.all_gather(whole, axes[number], axis=dim, tiled=True)
    return whole


def in_blocks(array, dim, peers):
    before, after = (array.shape[:dim], array.shape[dim + 1 :])
    return jnp.moveaxis(array.reshape(*before, peers, -1, *after), dim, 0)


def summed_on_arrival(array, axis, dim):
    blocks = in_blocks(array, dim, lax.axis_size(axis))
    arrived = lax.all_to_all(blocks, axis, split_axis=0, concat_axis=0, tiled=True)
    return arrived.sum(axis=0)


def slot_places(expert_ids, modality, tile_counts, expert):
    capacity = MAXT * TILE
    places = jnp.full(expert_ids.shape, -1, jnp.int32)
    for kind in range(2):
        member = ((expert_ids == expert) & (modality == kind)).astype(jnp.int32)
        rank = jnp.cumsum(member, dtype=jnp.int32) - 1
        limit = tile_counts[kind, expert] * TILE
        keep = (member == 1) & (rank < limit)
        places = jnp.where(keep, kind * capacity + rank, places)
    return places


def slot_table(places):
    slots = lax.broadcasted_iota(jnp.int32, (2 * MAXT * TILE, places.shape[0]), 0)
    return (slots == places[None, :]).astype(jnp.bfloat16)


def place_rows(places, values):
    index = jnp.maximum(places, 0)
    rows = jnp.take(values, index, axis=0)
    return jnp.where((places >= 0)[:, None], rows, jnp.zeros_like(rows))


def per_device(
    tokens,
    expert_ids,
    modality,
    tile_counts,
    router,
    w_gate,
    w_up,
    w_down,
    shared_gate,
    shared_up,
    shared_down,
):
    whole = whole_of(tokens, ROW, 0)
    expert = lax.axis_index("col")
    places = slot_places(expert_ids, modality, tile_counts, expert)
    table = slot_table(places)
    taken = jnp.dot(table, whole, preferred_element_type=jnp.float32).astype(jnp.bfloat16)
    score = jax.nn.sigmoid(jnp.dot(taken, router, preferred_element_type=jnp.float32))
    scaled = (taken.astype(jnp.float32) * score).astype(jnp.bfloat16)
    gate = jnp.dot(scaled, w_gate[0], preferred_element_type=jnp.float32)
    upper = jnp.dot(scaled, w_up[0], preferred_element_type=jnp.float32)
    hidden = (jax.nn.silu(gate) * upper).astype(jnp.bfloat16)
    result = jnp.dot(hidden, w_down[0], preferred_element_type=jnp.float32)
    width_row = shared_down.shape[1]
    feature_start = lax.axis_index(ROW) * width_row
    local_rows = lax.dynamic_slice_in_dim(whole, feature_start, width_row, 1)
    gate_part = jnp.dot(local_rows, shared_gate, preferred_element_type=jnp.float32)
    upper_part = jnp.dot(local_rows, shared_up, preferred_element_type=jnp.float32)
    shared_gate_sum, shared_up_sum = lax.psum((gate_part, upper_part), ROW)
    shared_hidden = (jax.nn.silu(shared_gate_sum) * shared_up_sum).astype(jnp.bfloat16)
    shared_part = jnp.dot(shared_hidden, shared_down, preferred_element_type=jnp.float32)
    slot_total = summed_on_arrival(result, ROW, 1)
    combined = place_rows(places, slot_total) + shared_part
    total = lax.psum_scatter(combined, "col", scatter_dimension=0, tiled=True)
    return total.astype(jnp.bfloat16)


def solution(mesh):
    split = Mesh(mesh.devices.reshape(4, 2, mesh.shape["col"]), ("row_0", "row_1", "col"))
    placed = (
        P(ROW, None),
        P(),
        P(),
        P(),
        P(None, "col"),
        P("col", None, ROW),
        P("col", None, ROW),
        P("col", ROW, None),
        P(ROW, "col"),
        P(ROW, "col"),
        P("col", ROW),
    )
    return jax.shard_map(
        per_device, mesh=split, in_specs=placed, out_specs=P("col", ROW), check_vma=False
    )
```

profile of v0, /device:TPU:25, one launch (start us, length us, event | category | flops | bytes accessed | tf_op | source)
XLA Modules:
  0.0 445.5 jit_solution(17335633771156441721)
XLA Ops:
  6.5 0.0 copy-start
  6.5 0.7 all-gather.3.cloned.1.call-update
  7.3 0.0 all-gather.5.cloned.1.call-start
  7.3 44.5 %all-gather.3.cloned.1.call-done = bf16[256,5120]{1,0:T(8,128)(2,1)} async-done(((bf16[128,5120]{1,0:T(8,128)(2,1)}), bf16[256,5120]{1,0:T(8,128)(2,1)}) %all-gather.3.cloned.1.call-update) | async-done | bytes 2621456 | tf_op jit(solution)/shard_map/all_gather | solution.py:15
  51.8 0.0 all-gather.5.cloned.1.call-update
  51.9 0.0 all-reduce.3.cloned.1.call-start
  51.9 104.0 %all-gather.5.cloned.1.call-done = bf16[1024,5120]{1,0:T(8,128)(2,1)} async-done(((bf16[256,5120]{1,0:T(8,128)(2,1)}), bf16[1024,5120]{1,0:T(8,128)(2,1)}) %all-gather.5.cloned.1.call-update) | async-done | bytes 10485776 | tf_op jit(solution)/shard_map/all_gather | solution.py:15
  155.9 3.6 fusion.4
  159.6 3.7 fusion.6
  163.2 0.0 all-reduce.3.cloned.1.call-update
  163.3 0.6 copy-done.5
  163.9 0.6 constant_dynamic-slice_fusion.1
  165.9 0.3 reduce-window.24
  166.2 0.1 slice.16
  166.3 0.3 reduce-window.16
  166.6 0.1 slice.14
  166.7 8.0 %copy.14 = bf16[5120,512]{1,0:T(8,128)(2,1)} copy(bf16[5120,512]{0,1:T(8,128)(2,1)} %bitcast.68) | data formatting | bytes 10485760 | tf_op jit(solution)/shard_map/dot_general | solution.py:76
  174.6 0.1 slice_reduce_fusion
  174.8 0.1 broadcast_compare_fusion
  174.9 5.9 %convolution_convert_fusion = bf16[64,5120]{1,0:T(8,128)(2,1)S(1)} fusion(bf16[1024,5120]{1,0:T(8,128)(2,1)} %all-gather.5.cloned.1.call-done, s32[1024]{0:T(1024)S(1)} %get-tuple-element.8), kind=kOutput, calls=%fused_computation.1 | convolution fusion | flops 671481856 | bytes 11145216 | tf_op jit(solution)/shard_map/dot_general | solution.py:70
  180.8 0.3 fusion.22
  181.1 3.6 fusion.2
  184.7 7.9 %convolution_bitcast_fusion = f32[8,64,640]{2,1,0:T(8,128)} fusion(bf16[8,640,512]{2,1,0:T(8,128)(2,1)} %bitcast.67, bf16[1,5120,512]{2,1,0:T(8,128)(2,1)} %param.17, bf16[64,5120]{1,0:T(8,128)(2,1)S(1)} %convolution_convert_fusion, f32[64]{0:T(128)S(1)} %fusion.22, f32[64,512]{1,0:T(8,128)S(1)} %fusion.2), kind=kOutput, calls=%fused_computation.8 | convolution fusion | flops 672268288 | bytes 12583168 | tf_op jit(solution)/shard_map/dot_general | solution.py:76
  192.6 4.9 %all-to-all-start = ((f32[8,64,640]{2,1,0:T(8,128)}), f32[8,64,640]{2,1,0:T(8,128)S(1)}, u32[]{:S(2)}, u32[]{:S(2)}) async-start(f32[8,64,640]{2,1,0:T(8,128)} %convolution_bitcast_fusion), calls=%async_computation | async-start | bytes 2621440 | tf_op jit(solution)/shard_map/all_to_all | solution.py:26
  197.5 24.8 %all-to-all-done = f32[8,64,640]{2,1,0:T(8,128)S(1)} async-done(((f32[8,64,640]{2,1,0:T(8,128)}), f32[8,64,640]{2,1,0:T(8,128)S(1)}, u32[]{:S(2)}, u32[]{:S(2)}) %all-to-all-start) | async-done | bytes 1310752 | tf_op jit(solution)/shard_map/all_to_all | solution.py:26
  222.3 0.1 reduce_sum.9
  222.4 3.8 gather_fusion
  226.1 133.4 %all-reduce.3.cloned.1.call-done = (f32[1024,512]{1,0:T(8,128)}, f32[1024,512]{1,0:T(8,128)}) async-done(((f32[1024,512]{1,0:T(8,128)}, f32[1024,512]{1,0:T(8,128)}), (f32[1024,512]{1,0:T(8,128)}, f32[1024,512]{1,0:T(8,128)})) %all-reduce.3.cloned.1.call-update) | async-done | bytes 4194320 | tf_op jit(solution)/shard_map/psum | solution.py:82
  359.5 4.9 %select_add_fusion = f32[1024,640]{1,0:T(8,128)} fusion(f32[1024,640]{1,0:T(8,128)S(1)} %gather_fusion, bf16[512,640]{1,0:T(8,128)(2,1)S(1)} %copy-done, pred[1024]{0:T(1024)(128)(4,1)S(1)} %maximum_compare_fusion, pred[1024]{0:T(1024)(128)(4,1)S(1)} %get-tuple-element.7, f32[1024,512]{1,0:T(8,128)} %get-tuple-element.5, f32[1024,512]{1,0:T(8,128)} %get-tuple-element.6), kind=kOutput, calls=%fused_computation.6 | convolution fusion | flops 676200448 | bytes 10094592 | tf_op jit(solution)/shard_map/dot_general | solution.py:84
  364.4 0.0 reduce-scatter.2.cloned.1.call-update
  364.5 72.9 %reduce-scatter.2.cloned.1.call-done = f32[64,640]{1,0:T(8,128)} async-done(((f32[1024,640]{1,0:T(8,128)}), f32[64,640]{1,0:T(8,128)}) %reduce-scatter.2.cloned.1.call-update) | async-done | bytes 163856 | tf_op jit(solution)/shard_map/reduce_scatter | solution.py:87
  437.4 1.6 convert_element_type.32
  (20 shorter events, 0.1 us)
Async XLA Ops:
  6.5 353.0 %copy-start = (bf16[512,640]{1,0:T(8,128)(2,1)S(1)}, bf16[512,640]{1,0:T(8,128)(2,1)}, u32[]{:S(2)}) copy-start(bf16[512,640]{1,0:T(8,128)(2,1)} %param.21) | copy-start | bytes 1966084
  6.5 149.4 %copy-start.1 = (bf16[640,512]{1,0:T(8,128)(2,1)S(1)}, bf16[640,512]{1,0:T(8,128)(2,1)}, u32[]{:S(2)}) copy-start(bf16[640,512]{1,0:T(8,128)(2,1)} %param.20) | copy-start | bytes 1966084
  6.5 45.3 %all-gather.3.cloned.1.call-start = ((), (), s32[]{:S(2)}) async-start(), calls=%async_computation.2 | async-start | bytes 3932160 | tf_op jit(solution)/shard_map/all_gather | solution.py:15
  7.3 148.7 %all-gather.5.cloned.1.call-start = ((), (), s32[]{:S(2)}) async-start(), calls=%async_computation.3 | async-start | bytes 13107200 | tf_op jit(solution)/shard_map/all_gather | solution.py:15
  51.9 107.7 %copy-start.2 = (bf16[640,512]{1,0:T(8,128)(2,1)S(1)}, bf16[640,512]{1,0:T(8,128)(2,1)}, u32[]{:S(2)}) copy-start(bf16[640,512]{1,0:T(8,128)(2,1)} %param.19) | copy-start | bytes 1966084
  51.9 307.7 %all-reduce.3.cloned.1.call-start = ((), (), s32[]{:S(2)}) async-start(), calls=%async_computation.5 | async-start | bytes 8388608 | tf_op jit(solution)/shard_map/psum | solution.py:82
  163.2 0.7 copy-start.5
  163.2 2.6 copy-start.3
  163.2 2.7 copy-start.4
  174.9 5.9 %copy-start.6 = (bf16[5120,1]{0,1:T(2,128)(2,1)S(1)}, bf16[5120,1]{0,1:T(2,128)(2,1)}, u32[]{:S(2)}) copy-start(bf16[5120,1]{0,1:T(2,128)(2,1)} %param.15) | copy-start | bytes 30724
  192.6 29.7 %all-to-all-start = ((f32[8,64,640]{2,1,0:T(8,128)}), f32[8,64,640]{2,1,0:T(8,128)S(1)}, u32[]{:S(2)}, u32[]{:S(2)}) async-start(f32[8,64,640]{2,1,0:T(8,128)} %convolution_bitcast_fusion), calls=%async_computation | async-start | bytes 2621440 | tf_op jit(solution)/shard_map/all_to_all | solution.py:26
  197.5 239.9 %reduce-scatter.2.cloned.1.call-start = ((), (), s32[]{:S(2)}) async-start(), calls=%async_computation.4 | async-start | bytes 2785280 | tf_op jit(solution)/shard_map/reduce_scatter | solution.py:87
Sparse Core Ops, SparseCore 0:
  9.0 42.8 all-gather.2
  53.5 102.3 all-gather.4
  163.4 196.0 all-reduce.2
  364.6 72.7 reduce-scatter.1
where the time goes:
time: 449 us; the launch traced here: 445 us
  waiting for transfers between devices  380 us (85%)
  matrix products  29.9 us (7%)
  between operations  14.5 us (3%)
  local copies, waits for them, and re-layouts  13.3 us (3%)
  starting transfers between devices  4.95 us (1%)
    all_gather x2, waiting for transfers between devices, whole_of(): whole = lax.all_gather(whole, axes[number], axis=dim, tiled=True)  149 us
    psum x1, waiting for transfers between devices, per_device(): shared_gate_sum, shared_up_sum = lax.psum((gate_part, upper_part), ROW)  133 us
    reduce_scatter x1, waiting for transfers between devices, per_device(): total = lax.psum_scatter(combined, 'col', scatter_dimension=0, tiled=True)  72.9 us
    all_to_all x1, waiting for transfers between devices, summed_on_arrival(): lax.all_to_all(blocks, axis, split_axis=0, concat_axis=0, tiled=True)  24.8 us
  transfers between devices with their start and end apart: 5, of which 5 were waited for; matrix products, arithmetic and copies ran while one was open for 7% of the time, Pallas kernels for 0%

commit v1 on v0

v1 whole, which is shorter than its diff:
```python
import jax
import jax.numpy as jnp
from jax import lax
from jax.experimental import pallas as pl
from jax.experimental.pallas import tpu as pltpu
from jax.sharding import Mesh
from jax.sharding import PartitionSpec as P

TILE = 8
MAXT = 4
ROW = ("x", "yl")
COL = ("yh", "z", "core")
ROWS = 8
MESH = pl.DeviceIdType.MESH
BF16 = jnp.bfloat16
F32 = jnp.float32


def dot(a, b):
    return jnp.dot(a, b, preferred_element_type=F32)


def silu(v):
    return v / (1.0 + jnp.exp(-v))


def kernel(
    ids, mod, counts, tokens, router, w_gate, w_up, w_down, s_gate, s_up, s_down,
    out,
    wg, wu, wd, sg, su, sd, xs, table, place, ysend, yrecv, xsend, xrecv, taken,
    hid_e, esend, erecv, eysend, eyrecv, hilo, hid, acc, sib, zsend, zrecv, hsend, hrecv,
    load_sem, a_send, a_recv, s_send, s_recv, y_send, y_recv, x_send, x_recv, b_send, b_recv,
    e_send, e_recv, ey_send, ey_recv, d_send, d_recv, k_send, k_recv, z_send, z_recv, h_send, h_recv,
):
    x, yl, yh = lax.axis_index("x"), lax.axis_index("yl"), lax.axis_index("yh")
    z, core = lax.axis_index("z"), lax.axis_index("core")
    block, width = xs.shape[1], xs.shape[2]
    half = block // 2
    slots = table.shape[0]
    hidden = sg.shape[1]
    row = x * 2 + yl
    expert = yh * 8 + z * 2 + core

    def ahead(dx):
        return lax.rem(x + dx, 4)

    def owner(slot):
        dx, dy = slot // 2, slot % 2
        return lax.rem(x + 4 - dx, 4) * 2 + (yl + dy) % 2

    def to_row(dx, dy):
        return {"x": ahead(dx), "yl": lax.rem(yl + dy, 2)}

    sibling = {"core": 1 - core}
    other_y = {"yl": 1 - yl}

    def remote(src, dst, send, recv, device):
        return pltpu.make_async_remote_copy(
            src_ref=src, dst_ref=dst, send_sem=send, recv_sem=recv, device_id=device, device_id_type=MESH
        )

    loads = [
        pltpu.make_async_copy(tokens.at[:, pl.ds(pl.multiple_of(row * width, 128), width)], xs.at[0], load_sem.at[0]),
        pltpu.make_async_copy(s_gate, sg, load_sem.at[1]),
        pltpu.make_async_copy(s_up, su, load_sem.at[2]),
        pltpu.make_async_copy(w_gate.at[0], wg, load_sem.at[3]),
        pltpu.make_async_copy(w_up.at[0], wu, load_sem.at[4]),
        pltpu.make_async_copy(w_down.at[0], wd, load_sem.at[5]),
        pltpu.make_async_copy(s_down, sd, load_sem.at[6]),
    ]
    for load in loads:
        load.start()

    barrier = pltpu.get_barrier_semaphore()
    peers = [to_row(s // 2, s % 2) for s in range(1, ROWS)]
    peers += [{"z": lax.rem(z + dz, 4)} for dz in (1, 2, 3)] + [{"yh": 1 - yh}, sibling]
    for peer in peers:
        pl.semaphore_signal(barrier, inc=1, device_id=peer, device_id_type=MESH)

    count = ids.shape[1]
    lane = lax.broadcasted_iota(jnp.int32, (2, count), 1)
    kind = lax.broadcasted_iota(jnp.int32, (2, count), 0)
    member = (ids[...] == expert) & (mod[...] == kind)
    rank = member.astype(jnp.int32)
    step = 1
    while step < count:
        rank = rank + jnp.where(lane >= step, pltpu.roll(rank, step, 1), 0)
        step *= 2
    rank = rank - 1
    limit = jnp.where(kind == 0, counts[0, expert], counts[1, expert]) * TILE
    keep = member & (rank < limit)
    spot = jnp.where(keep, kind * (MAXT * TILE) + rank, -1)
    places = jnp.maximum(spot[0:1, :], spot[1:2, :])
    at = lax.broadcasted_iota(jnp.int32, (slots, count), 0)
    ones = (at == places).astype(F32)
    table[...] = ones.astype(BF16)
    double = jnp.concatenate([ones, ones], axis=0)
    place[...] = double.T.astype(BF16)

    pl.semaphore_wait(barrier, len(peers))

    mine = pl.ds(pl.multiple_of(core * half, half), half)
    his = pl.ds(pl.multiple_of((1 - core) * half, half), half)

    def a_copy(s):
        dx, dy = s // 2, s % 2
        target = ahead(dx) * 2 + lax.rem(yl + dy, 2)
        return remote(
            tokens.at[mine, pl.ds(pl.multiple_of(target * width, 128), width)],
            xs.at[s, mine], a_send.at[s], a_recv.at[s], to_row(dx, dy),
        )

    def s_copy(s):
        return remote(xs.at[s, mine], xs.at[s, mine], s_send.at[s], s_recv.at[s], sibling)

    def s_arrival(s):
        return remote(xs.at[s, his], xs.at[s, his], s_send.at[s], s_recv.at[s], sibling)

    order = (1, 3, 7, 5, 4, 2, 6)
    for s in order:
        a_copy(s).start()
    loads[0].wait()
    loads[1].wait()
    loads[2].wait()

    def y_copy(dx):
        return remote(ysend.at[dx], yrecv.at[dx], y_send.at[dx], y_recv.at[dx], other_y)

    def x_copy(dx):
        return remote(xsend.at[dx - 1], xrecv.at[dx - 1], x_send.at[dx - 1], x_recv.at[dx - 1], {"x": ahead(4 - dx)})

    for s in order:
        a_copy(s).wait_recv()
        s_copy(s).start()
        if s % 2 == 1:
            s_arrival(s).wait_recv()
            ysend[s // 2, :, :hidden] = dot(xs[s], sg[...]).astype(BF16)
            ysend[s // 2, :, hidden:] = dot(xs[s], su[...]).astype(BF16)
            y_copy(s // 2).start()
    for s in (4, 2, 6):
        s_arrival(s).wait_recv()

    def part_of(s):
        columns = pl.ds(pl.multiple_of(owner(s) * block, 128), block)
        return dot(table[:, columns], xs[s])

    rows = part_of(0)
    for s in range(1, ROWS):
        rows = rows + part_of(s)
    taken[0] = rows.astype(BF16)

    def b_copy(source, dx, dy):
        s = dx * 2 + dy if source == 0 else dx * 2 + 1
        return remote(taken.at[source], taken.at[s], b_send.at[s], b_recv.at[s], to_row(dx, dy))

    b_out = [b_copy(0, 0, 1), b_copy(0, 2, 0), b_copy(0, 1, 0), b_copy(0, 3, 0)]
    for copy in b_out:
        copy.start()

    def pair_sum(dx):
        y_copy(dx).wait_recv()
        s = dx * 2
        gate = dot(xs[s], sg[...]) + yrecv[dx, :, :hidden].astype(F32)
        upper = dot(xs[s], su[...]) + yrecv[dx, :, hidden:].astype(F32)
        return gate, upper

    def pair_send(dx):
        gate, upper = pair_sum(dx)
        xsend[dx - 1, :, :hidden] = gate.astype(BF16)
        xsend[dx - 1, :, hidden:] = upper.astype(BF16)
        x_copy(dx).start()

    def b_arrival(s):
        return remote(taken.at[s], taken.at[s], b_send.at[s], b_recv.at[s], other_y)

    b_arrival(1).wait_recv()
    relayed = [b_copy(1, dx, 0) for dx in (2, 1, 3)]
    for copy in relayed:
        copy.start()
    b_out += relayed
    pair_send(2)
    pair_send(1)

    for s in (2, 3, 4, 5, 6, 7):
        b_arrival(s).wait_recv()
    loads[3].wait()
    loads[4].wait()

    def score_part(s, total):
        line = router[:, pl.ds(pl.multiple_of(owner(s) * width, 128), width)].astype(F32)
        return total + jnp.sum(taken[s].astype(F32) * line, axis=1, keepdims=True)

    logit = lax.fori_loop(0, ROWS, score_part, jnp.zeros((slots, 1), F32))
    score = 1.0 / (1.0 + jnp.exp(-logit))

    def expert_part(s, sums):
        gate, upper = sums
        scaled = (taken[s].astype(F32) * score).astype(BF16)
        features = pl.ds(pl.multiple_of(owner(s) * width, 128), width)
        return gate + dot(scaled, wg[features, :]), upper + dot(scaled, wu[features, :])

    zero = jnp.zeros((slots, wg.shape[1]), F32)
    gate, upper = lax.fori_loop(0, ROWS, expert_part, (zero, zero))
    hid_e[...] = (silu(gate) * upper).astype(BF16)
    pair_send(3)
    loads[5].wait()

    def result_part(dx, dy):
        target = ahead(dx) * 2 + lax.rem(yl + dy, 2)
        return dot(hid_e[...], wd[:, pl.ds(pl.multiple_of(target * width, 128), width)])

    def e_copy(dx):
        return remote(esend.at[dx - 1], erecv.at[dx - 1], e_send.at[dx - 1], e_recv.at[dx - 1], {"x": ahead(dx)})

    for dx in (2, 1, 3):
        esend[dx - 1, 0] = result_part(dx, 0).astype(BF16)
        esend[dx - 1, 1] = result_part(dx, 1).astype(BF16)
        e_copy(dx).start()

    gate, upper = pair_sum(0)
    for dx in (2, 1, 3):
        x_copy(dx).wait_recv()
        gate = gate + xrecv[dx - 1, :, :hidden].astype(F32)
        upper = upper + xrecv[dx - 1, :, hidden:].astype(F32)
    hid[0] = (silu(gate) * upper).astype(BF16)

    def d_copy(source, dx, dy):
        s = dx * 2 + dy if source == 0 else dx * 2 + 1
        return remote(hid.at[source], hid.at[s], d_send.at[s], d_recv.at[s], to_row(dx, dy))

    def d_arrival(s):
        return remote(hid.at[s], hid.at[s], d_send.at[s], d_recv.at[s], other_y)

    d_out = [d_copy(0, 0, 1), d_copy(0, 2, 0), d_copy(0, 1, 0), d_copy(0, 3, 0)]
    for copy in d_out:
        copy.start()

    total = result_part(0, 0)
    passed = result_part(0, 1)
    for dx in (2, 1, 3):
        e_copy(dx).wait_recv()
        total = total + erecv[dx - 1, 0].astype(F32)
        passed = passed + erecv[dx - 1, 1].astype(F32)
    eysend[...] = passed.astype(BF16)
    ey_copy = remote(eysend, eyrecv, ey_send, ey_recv, other_y)
    ey_copy.start()
    d_arrival(1).wait_recv()
    relayed = [d_copy(1, dx, 0) for dx in (2, 1, 3)]
    for copy in relayed:
        copy.start()
    d_out += relayed
    ey_copy.wait_recv()
    total = total + eyrecv[...].astype(F32)
    high = total.astype(BF16)
    hilo[:slots] = high
    hilo[slots:] = (total - high.astype(F32)).astype(BF16)
    loads[6].wait()

    def k_copy(s):
        j = owner(s)
        return remote(acc.at[j, his], sib.at[j], k_send.at[s], k_recv.at[s], sibling)

    arrivals = (0, 1, 2, 6, 4, 3, 7, 5)
    for s in arrivals:
        if s > 1:
            d_arrival(s).wait_recv()
        j = owner(s)
        tokens_of = pl.ds(pl.multiple_of(j * block, 128), block)
        acc[j] = dot(hid[s], sd[...]) + dot(place[tokens_of, :], hilo[...])
        k_copy(s).start()
    for s in arrivals:
        k_copy(s).wait_recv()

    def chip_sum(dz, dyh):
        j = lax.rem(yh + dyh, 2) * 4 + lax.rem(z + dz, 4)
        return acc[j, mine] + sib[j]

    def z_copy(dz):
        return remote(
            zsend.at[dz - 1], zrecv.at[dz - 1], z_send.at[dz - 1], z_recv.at[dz - 1], {"z": lax.rem(z + dz, 4)}
        )

    for dz in (2, 1, 3):
        zsend[dz - 1, 0] = chip_sum(dz, 0).astype(BF16)
        zsend[dz - 1, 1] = chip_sum(dz, 1).astype(BF16)
        z_copy(dz).start()
    total = chip_sum(0, 0)
    passed = chip_sum(0, 1)
    for dz in (2, 1, 3):
        z_copy(dz).wait_recv()
        total = total + zrecv[dz - 1, 0].astype(F32)
        passed = passed + zrecv[dz - 1, 1].astype(F32)
    hsend[...] = passed.astype(BF16)
    h_copy = remote(hsend, hrecv, h_send, h_recv, {"yh": 1 - yh})
    h_copy.start()
    h_copy.wait_recv()
    out[...] = (total + hrecv[...].astype(F32)).astype(BF16)

    for s in order:
        a_copy(s).wait_send()
        s_copy(s).wait_send()
    for dx in range(4):
        y_copy(dx).wait_send()
    for dx in (1, 2, 3):
        x_copy(dx).wait_send()
        e_copy(dx).wait_send()
        z_copy(dx).wait_send()
    for copy in b_out + d_out:
        copy.wait_send()
    for s in arrivals:
        k_copy(s).wait_send()
    ey_copy.wait_send()
    h_copy.wait_send()


def per_device(tokens, expert_ids, modality, tile_counts, router, w_gate, w_up, w_down, shared_gate, shared_up, shared_down):
    block, depth = tokens.shape
    width = shared_down.shape[1]
    hidden = shared_gate.shape[1]
    inner = w_gate.shape[2]
    slots = 2 * MAXT * TILE
    half = block // 2
    count = expert_ids.shape[0]
    vmem = pl.BlockSpec(memory_space=pltpu.VMEM)
    hbm = pl.BlockSpec(memory_space=pl.ANY)
    dma = pltpu.SemaphoreType.DMA
    return pl.pallas_call(
        kernel,
        name="layer",
        out_shape=jax.ShapeDtypeStruct((half, width), BF16),
        in_specs=[vmem, vmem, pl.BlockSpec(memory_space=pltpu.SMEM), hbm, vmem] + [hbm] * 6,
        out_specs=vmem,
        scratch_shapes=[
            pltpu.VMEM((depth, inner), BF16),
            pltpu.VMEM((depth, inner), BF16),
            pltpu.VMEM((inner, depth), BF16),
            pltpu.VMEM((width, hidden), BF16),
            pltpu.VMEM((width, hidden), BF16),
            pltpu.VMEM((hidden, width), BF16),
            pltpu.VMEM((ROWS, block, width), BF16),
            pltpu.VMEM((slots, count), BF16),
            pltpu.VMEM((count, 2 * slots), BF16),
            pltpu.VMEM((4, block, 2 * hidden), BF16),
            pltpu.VMEM((4, block, 2 * hidden), BF16),
            pltpu.VMEM((3, block, 2 * hidden), BF16),
            pltpu.VMEM((3, block, 2 * hidden), BF16),
            pltpu.VMEM((ROWS, slots, width), BF16),
            pltpu.VMEM((slots, inner), BF16),
            pltpu.VMEM((3, 2, slots, width), BF16),
            pltpu.VMEM((3, 2, slots, width), BF16),
            pltpu.VMEM((slots, width), BF16),
            pltpu.VMEM((slots, width), BF16),
            pltpu.VMEM((2 * slots, width), BF16),
            pltpu.VMEM((ROWS, block, hidden), BF16),
            pltpu.VMEM((ROWS, block, width), F32),
            pltpu.VMEM((ROWS, half, width), F32),
            pltpu.VMEM((3, 2, half, width), BF16),
            pltpu.VMEM((3, 2, half, width), BF16),
            pltpu.VMEM((half, width), BF16),
            pltpu.VMEM((half, width), BF16),
            dma((7,)),
            dma((ROWS,)), dma((ROWS,)), dma((ROWS,)), dma((ROWS,)),
            dma((4,)), dma((4,)), dma((3,)), dma((3,)),
            dma((ROWS,)), dma((ROWS,)),
            dma((3,)), dma((3,)), dma, dma,
            dma((ROWS,)), dma((ROWS,)), dma((ROWS,)), dma((ROWS,)),
            dma((3,)), dma((3,)), dma, dma,
        ],
        compiler_params=pltpu.CompilerParams(
            collective_id=0, has_side_effects=True, vmem_limit_bytes=60 * 1024 * 1024
        ),
    )(
        expert_ids.reshape(1, count), modality.reshape(1, count), tile_counts, tokens, router.reshape(1, depth),
        w_gate, w_up, w_down, shared_gate, shared_up, shared_down,
    )


def solution(mesh):
    split = Mesh(mesh.devices.reshape(4, 2, 2, 4, 2), ("x", "yl", "yh", "z", "core"))
    placed = (
        P(ROW, None),
        P(),
        P(),
        P(),
        P(None, COL),
        P(COL, None, ROW),
        P(COL, None, ROW),
        P(COL, ROW, None),
        P(ROW, COL),
        P(ROW, COL),
        P(COL, ROW),
    )
    return jax.shard_map(
        per_device, mesh=split, in_specs=placed, out_specs=P(COL, ROW), check_vma=False
    )
```

time: 449 us -> 104 us (0.23)
  the two profiles are of different devices: /device:TPU:25 before, /device:TPU:1 now
where the time goes in v1:
time: 104 us; the launch traced here: 103 us
  Pallas kernels  102 us (98%)
  local copies, waits for them, and re-layouts  1.53 us (1%)
    pallas_call x1, Pallas kernels, per_device(): pl.pallas_call(kernel, name='layer', out_shape=jax.ShapeDtypeStruct((half...  102 us

profile of v1, /device:TPU:1, one launch (start us, length us, event | category | flops | bytes accessed | tf_op | source)
XLA Modules:
  0.0 103.3 jit_solution(13819742820942184599)
XLA Ops:
  0.0 101.8 %layer.1 = bf16[64,640]{1,0:T(8,128)(2,1)} custom-call(s32[1,1024]{1,0:T(1,128)} %bitcast.4, s32[1,1024]{1,0:T(1,128)} %bitcast.5, s32[2,16]{1,0:T(2,128)} %counts.1, bf16[128,5120]{1,0:T(8,128)(2,1)} %tokens.1, bf16[1,5120]{1,0:T(2,128)(2,1)} %bitcast.3, bf16[1,5120,512]{2,1,0:T(8,128)(2,1)} %w_gate.1, bf16[1,5120,512]{2,1,0:T(8,128)(2,1)} %w_up.1, ...), custom_call_target="tpu_custom_call" | custom-call | tf_op jit(solution)/shard_map/layer/pallas_call | solution.py:327
  101.8 1.5 %copy.13 = bf16[64,640]{1,0:T(8,128)(2,1)} copy(bf16[64,640]{1,0:T(8,128)(2,1)} %layer.1) | data formatting | bytes 163840

commit v2 on v1

--- a/solution.py
+++ b/solution.py
@@ -28,7 +28,7 @@
     ids, mod, counts, tokens, router, w_gate, w_up, w_down, s_gate, s_up, s_down,
     out,
     wg, wu, wd, sg, su, sd, xs, table, place, ysend, yrecv, xsend, xrecv, taken,
-    hid_e, esend, erecv, eysend, eyrecv, hilo, hid, acc, sib, zsend, zrecv, hsend, hrecv,
+    hid_e, esend, erecv, eysend, eyrecv, hilo, hid, acc, sib, own, zsend, zrecv, hsend, hrecv,
     load_sem, a_send, a_recv, s_send, s_recv, y_send, y_recv, x_send, x_recv, b_send, b_recv,
     e_send, e_recv, ey_send, ey_recv, d_send, d_recv, k_send, k_recv, z_send, z_recv, h_send, h_recv,
 ):
@@ -116,12 +116,10 @@
     def s_arrival(s):
         return remote(xs.at[s, his], xs.at[s, his], s_send.at[s], s_recv.at[s], sibling)
 
-    order = (1, 3, 7, 5, 4, 2, 6)
+    order = (5, 3, 7, 1, 4, 2, 6)
     for s in order:
         a_copy(s).start()
     loads[0].wait()
-    loads[1].wait()
-    loads[2].wait()
 
     def y_copy(dx):
         return remote(ysend.at[dx], yrecv.at[dx], y_send.at[dx], y_recv.at[dx], other_y)
@@ -132,20 +130,14 @@
     for s in order:
         a_copy(s).wait_recv()
         s_copy(s).start()
-        if s % 2 == 1:
-            s_arrival(s).wait_recv()
-            ysend[s // 2, :, :hidden] = dot(xs[s], sg[...]).astype(BF16)
-            ysend[s // 2, :, hidden:] = dot(xs[s], su[...]).astype(BF16)
-            y_copy(s // 2).start()
-    for s in (4, 2, 6):
-        s_arrival(s).wait_recv()
 
     def part_of(s):
         columns = pl.ds(pl.multiple_of(owner(s) * block, 128), block)
         return dot(table[:, columns], xs[s])
 
     rows = part_of(0)
-    for s in range(1, ROWS):
+    for s in order:
+        s_arrival(s).wait_recv()
         rows = rows + part_of(s)
     taken[0] = rows.astype(BF16)
 
@@ -153,9 +145,26 @@
         s = dx * 2 + dy if source == 0 else dx * 2 + 1
         return remote(taken.at[source], taken.at[s], b_send.at[s], b_recv.at[s], to_row(dx, dy))
 
+    def b_arrival(s):
+        return remote(taken.at[s], taken.at[s], b_send.at[s], b_recv.at[s], other_y)
+
     b_out = [b_copy(0, 0, 1), b_copy(0, 2, 0), b_copy(0, 1, 0), b_copy(0, 3, 0)]
     for copy in b_out:
         copy.start()
+
+    loads[1].wait()
+    loads[2].wait()
+    for dx in (2, 1, 3, 0):
+        s = dx * 2 + 1
+        ysend[dx, :, :hidden] = dot(xs[s], sg[...]).astype(BF16)
+        ysend[dx, :, hidden:] = dot(xs[s], su[...]).astype(BF16)
+        y_copy(dx).start()
+
+    b_arrival(1).wait_recv()
+    relayed = [b_copy(1, dx, 0) for dx in (2, 1, 3)]
+    for copy in relayed:
+        copy.start()
+    b_out += relayed
 
     def pair_sum(dx):
         y_copy(dx).wait_recv()
@@ -170,14 +179,6 @@
         xsend[dx - 1, :, hidden:] = upper.astype(BF16)
         x_copy(dx).start()
 
-    def b_arrival(s):
-        return remote(taken.at[s], taken.at[s], b_send.at[s], b_recv.at[s], other_y)
-
-    b_arrival(1).wait_recv()
-    relayed = [b_copy(1, dx, 0) for dx in (2, 1, 3)]
-    for copy in relayed:
-        copy.start()
-    b_out += relayed
     pair_send(2)
     pair_send(1)
 
@@ -257,42 +258,53 @@
     loads[6].wait()
 
     def k_copy(s):
+        return remote(acc.at[s, his], sib.at[s], k_send.at[s], k_recv.at[s], sibling)
+
+    def place_of(s):
         j = owner(s)
-        return remote(acc.at[j, his], sib.at[j], k_send.at[s], k_recv.at[s], sibling)
-
-    arrivals = (0, 1, 2, 6, 4, 3, 7, 5)
-    for s in arrivals:
+        return lax.rem(lax.rem(j, 4) + 4 - z, 4), lax.rem(j // 4 + yh, 2)
+
+    def z_copy(dz, dyh, s):
+        return remote(
+            zsend.at[s], zrecv.at[dz - 1, dyh], z_send.at[dz - 1, dyh], z_recv.at[dz - 1, dyh], {"z": lax.rem(z + dz, 4)}
+        )
+
+    def pass_on(s):
+        k_copy(s).wait_recv()
+        dz, dyh = place_of(s)
+        total = acc[s, mine] + sib[s]
+
+        @pl.when(dz == 0)
+        def _():
+            own[dyh] = total
+
+        @pl.when(dz > 0)
+        def _():
+            zsend[s] = total.astype(BF16)
+            z_copy(dz, dyh, s).start()
+
+    arrivals = (0, 1, 4, 2, 6, 5, 3, 7)
+    for i, s in enumerate(arrivals):
         if s > 1:
             d_arrival(s).wait_recv()
-        j = owner(s)
-        tokens_of = pl.ds(pl.multiple_of(j * block, 128), block)
-        acc[j] = dot(hid[s], sd[...]) + dot(place[tokens_of, :], hilo[...])
+        tokens_of = pl.ds(pl.multiple_of(owner(s) * block, 128), block)
+        acc[s] = dot(hid[s], sd[...]) + dot(place[tokens_of, :], hilo[...])
         k_copy(s).start()
-    for s in arrivals:
-        k_copy(s).wait_recv()
-
-    def chip_sum(dz, dyh):
-        j = lax.rem(yh + dyh, 2) * 4 + lax.rem(z + dz, 4)
-        return acc[j, mine] + sib[j]
-
-    def z_copy(dz):
-        return remote(
-            zsend.at[dz - 1], zrecv.at[dz - 1], z_send.at[dz - 1], z_recv.at[dz - 1], {"z": lax.rem(z + dz, 4)}
-        )
-
-    for dz in (2, 1, 3):
-        zsend[dz - 1, 0] = chip_sum(dz, 0).astype(BF16)
-        zsend[dz - 1, 1] = chip_sum(dz, 1).astype(BF16)
-        z_copy(dz).start()
-    total = chip_sum(0, 0)
-    passed = chip_sum(0, 1)
-    for dz in (2, 1, 3):
-        z_copy(dz).wait_recv()
-        total = total + zrecv[dz - 1, 0].astype(F32)
-        passed = passed + zrecv[dz - 1, 1].astype(F32)
-    hsend[...] = passed.astype(BF16)
+        if i > 0:
+            pass_on(arrivals[i - 1])
+    pass_on(arrivals[-1])
+
+    def z_sum(dyh):
+        total = own[dyh]
+        for dz in (1, 2, 3):
+            z_copy(dz, dyh, 0).wait_recv()
+            total = total + zrecv[dz - 1, dyh].astype(F32)
+        return total
+
+    hsend[...] = z_sum(1).astype(BF16)
     h_copy = remote(hsend, hrecv, h_send, h_recv, {"yh": 1 - yh})
     h_copy.start()
+    total = z_sum(0)
     h_copy.wait_recv()
     out[...] = (total + hrecv[...].astype(F32)).astype(BF16)
 
@@ -304,7 +316,8 @@
     for dx in (1, 2, 3):
         x_copy(dx).wait_send()
         e_copy(dx).wait_send()
-        z_copy(dx).wait_send()
+        z_copy(dx, 0, 0).wait_send()
+        z_copy(dx, 1, 0).wait_send()
     for copy in b_out + d_out:
         copy.wait_send()
     for s in arrivals:
@@ -354,7 +367,8 @@
             pltpu.VMEM((ROWS, block, hidden), BF16),
             pltpu.VMEM((ROWS, block, width), F32),
             pltpu.VMEM((ROWS, half, width), F32),
-            pltpu.VMEM((3, 2, half, width), BF16),
+            pltpu.VMEM((2, half, width), F32),
+            pltpu.VMEM((ROWS, half, width), BF16),
             pltpu.VMEM((3, 2, half, width), BF16),
             pltpu.VMEM((half, width), BF16),
             pltpu.VMEM((half, width), BF16),
@@ -364,7 +378,7 @@
             dma((ROWS,)), dma((ROWS,)),
             dma((3,)), dma((3,)), dma, dma,
             dma((ROWS,)), dma((ROWS,)), dma((ROWS,)), dma((ROWS,)),
-            dma((3,)), dma((3,)), dma, dma,
+            dma((3, 2)), dma((3, 2)), dma, dma,
         ],
         compiler_params=pltpu.CompilerParams(
             collective_id=0, has_side_effects=True, vmem_limit_bytes=60 * 1024 * 1024

time: 104 us -> 83 us (0.80)
  the two profiles are of different devices: /device:TPU:1 before, /device:TPU:26 now
where the time goes in v2:
time: 83 us; the launch traced here: 82.8 us
  Pallas kernels  81.2 us (98%)
  local copies, waits for them, and re-layouts  1.53 us (2%)
    pallas_call x1, Pallas kernels, per_device(): pl.pallas_call(kernel, name='layer', out_shape=jax.ShapeDtypeStruct((half...  81.2 us

profile of v2, /device:TPU:26, one launch (start us, length us, event | category | flops | bytes accessed | tf_op | source)
XLA Modules:
  0.0 82.8 jit_solution(15216220213080033906)
XLA Ops:
  0.0 81.2 %layer.1 = bf16[64,640]{1,0:T(8,128)(2,1)} custom-call(s32[1,1024]{1,0:T(1,128)} %bitcast.4, s32[1,1024]{1,0:T(1,128)} %bitcast.5, s32[2,16]{1,0:T(2,128)} %counts.1, bf16[128,5120]{1,0:T(8,128)(2,1)} %tokens.1, bf16[1,5120]{1,0:T(2,128)(2,1)} %bitcast.3, bf16[1,5120,512]{2,1,0:T(8,128)(2,1)} %w_gate.1, bf16[1,5120,512]{2,1,0:T(8,128)(2,1)} %w_up.1, ...), custom_call_target="tpu_custom_call" | custom-call | tf_op jit(solution)/shard_map/layer/pallas_call | solution.py:340
  81.2 1.5 %copy.13 = bf16[64,640]{1,0:T(8,128)(2,1)} copy(bf16[64,640]{1,0:T(8,128)(2,1)} %layer.1) | data formatting | bytes 163840

commit v3 on v1

v3 whole, which is shorter than its diff:
```python
import jax
import jax.numpy as jnp
from jax import lax
from jax.experimental import pallas as pl
from jax.experimental.pallas import tpu as pltpu
from jax.sharding import Mesh
from jax.sharding import PartitionSpec as P

TILE = 8
MAXT = 4
ROW = ("x", "yl")
COL = ("yh", "z", "core")
ROWS = 8
MESH = pl.DeviceIdType.MESH
BF16 = jnp.bfloat16
F32 = jnp.float32


def dot(a, b):
    return jnp.dot(a, b, preferred_element_type=F32)


def silu(v):
    return v / (1.0 + jnp.exp(-v))


def kernel(
    ids, mod, counts, tokens, router, w_gate, w_up, w_down, s_gate, s_up, s_down,
    out,
    wg, wu, wd, sg, su, sd, xs, table, place, ysend, yrecv, xsend, xrecv, taken,
    hid_e, eysend, eyrecv, exsend, exrecv, hilo, mine_h, hid, own, fsend, frecv,
    load_sem, a_send, a_recv, s_send, s_recv, y_send, y_recv, x_send, x_recv, b_send, b_recv,
    ey_send, ey_recv, ex_send, ex_recv, d_send, d_recv, w_send, w_recv, k_send, k_recv, f_send, f_recv,
):
    x, yl, yh = lax.axis_index("x"), lax.axis_index("yl"), lax.axis_index("yh")
    z, core = lax.axis_index("z"), lax.axis_index("core")
    block, width = xs.shape[1], xs.shape[2]
    half = block // 2
    slots = table.shape[0]
    chunk = mine_h.shape[2]
    row = x * 2 + yl
    expert = yh * 8 + z * 2 + core

    def ahead(dx):
        return lax.rem(x + dx, 4)

    def owner(slot):
        dx, dy = slot // 2, slot % 2
        return lax.rem(x + 4 - dx, 4) * 2 + (yl + dy) % 2

    def to_row(dx, dy):
        return {"x": ahead(dx), "yl": lax.rem(yl + dy, 2)}

    sibling = {"core": 1 - core}
    other_y = {"yl": 1 - yl}

    def remote(src, dst, send, recv, device):
        return pltpu.make_async_remote_copy(
            src_ref=src, dst_ref=dst, send_sem=send, recv_sem=recv, device_id=device, device_id_type=MESH
        )

    units = pl.ds(pl.multiple_of(core * chunk, chunk), chunk)

    loads = [
        pltpu.make_async_copy(tokens.at[:, pl.ds(pl.multiple_of(row * width, 128), width)], xs.at[0], load_sem.at[0]),
        pltpu.make_async_copy(s_gate, sg, load_sem.at[1]),
        pltpu.make_async_copy(s_up, su, load_sem.at[2]),
        pltpu.make_async_copy(w_gate.at[0], wg, load_sem.at[3]),
        pltpu.make_async_copy(w_up.at[0], wu, load_sem.at[4]),
        pltpu.make_async_copy(w_down.at[0], wd, load_sem.at[5]),
        pltpu.make_async_copy(s_down.at[:chunk], sd.at[0, units], load_sem.at[6]),
        pltpu.make_async_copy(s_down.at[chunk:], sd.at[1, units], load_sem.at[7]),
    ]
    for load in loads:
        load.start()

    barrier = pltpu.get_barrier_semaphore()
    peers = [to_row(s // 2, s % 2) for s in range(1, ROWS)]
    peers += [to_row(s // 2, s % 2) | sibling for s in (1, 2, 4, 6)] + [sibling]
    peers += [{"yh": lax.rem(yh + q // 4, 2), "z": lax.rem(z + q % 4, 4)} for q in range(1, 8)]
    for peer in peers:
        pl.semaphore_signal(barrier, inc=1, device_id=peer, device_id_type=MESH)

    count = ids.shape[1]
    lane = lax.broadcasted_iota(jnp.int32, (2, count), 1)
    kind = lax.broadcasted_iota(jnp.int32, (2, count), 0)
    at = lax.broadcasted_iota(jnp.int32, (slots, count), 0)

    def ones_of(expert):
        member = (ids[...] == expert) & (mod[...] == kind)
        rank = member.astype(jnp.int32)
        step = 1
        while step < count:
            rank = rank + jnp.where(lane >= step, pltpu.roll(rank, step, 1), 0)
            step *= 2
        rank = rank - 1
        limit = jnp.where(kind == 0, counts[0, expert], counts[1, expert]) * TILE
        spot = jnp.where(member & (rank < limit), kind * (MAXT * TILE) + rank, -1)
        return (at == jnp.maximum(spot[0:1, :], spot[1:2, :])).astype(F32)

    ones = ones_of(expert)
    table[...] = ones.astype(BF16)
    place[:, : 2 * slots] = jnp.concatenate([ones, ones], axis=0).T.astype(BF16)

    pl.semaphore_wait(barrier, len(peers))

    mine = pl.ds(pl.multiple_of(core * half, half), half)
    his = pl.ds(pl.multiple_of((1 - core) * half, half), half)

    def a_copy(s):
        dx, dy = s // 2, s % 2
        target = ahead(dx) * 2 + lax.rem(yl + dy, 2)
        return remote(
            tokens.at[mine, pl.ds(pl.multiple_of(target * width, 128), width)],
            xs.at[s, mine], a_send.at[s], a_recv.at[s], to_row(dx, dy),
        )

    def s_copy(s):
        return remote(xs.at[s, mine], xs.at[s, mine], s_send.at[s], s_recv.at[s], sibling)

    def s_arrival(s):
        return remote(xs.at[s, his], xs.at[s, his], s_send.at[s], s_recv.at[s], sibling)

    order = (5, 3, 7, 1, 4, 2, 6)
    for s in order:
        a_copy(s).start()
    loads[0].wait()

    def y_copy(q, dx):
        return remote(ysend.at[q, dx], yrecv.at[q, dx], y_send.at[q, dx], y_recv.at[q, dx], other_y)

    def x_copy(q, dx):
        return remote(
            xsend.at[q, dx - 1], xrecv.at[q, dx - 1], x_send.at[q, dx - 1], x_recv.at[q, dx - 1], {"x": ahead(4 - dx)}
        )

    w_out = [
        remote(s_down.at[q * chunk : (q + 1) * chunk], sd.at[q, units], w_send.at[q], w_recv.at[q], sibling)
        for q in (0, 1)
    ]
    for copy in w_out:
        copy.start()
    ones = ones_of(yh * 8 + z * 2 + 1 - core)
    place[:, 2 * slots :] = jnp.concatenate([ones, ones], axis=0).T.astype(BF16)

    def part(q, s):
        columns = slice(q * chunk, (q + 1) * chunk)
        return dot(xs[s], sg[:, columns]), dot(xs[s], su[:, columns])

    def y_start(q, dx):
        gate, upper = part(q, dx * 2 + 1)
        ysend[q, dx, :, :chunk] = gate.astype(BF16)
        ysend[q, dx, :, chunk:] = upper.astype(BF16)
        y_copy(q, dx).start()

    loads[1].wait()
    loads[2].wait()
    for s in order[:2]:
        a_copy(s).wait_recv()
        s_copy(s).start()
    s_arrival(order[0]).wait_recv()
    y_start(0, 2)
    for s in order[2:]:
        a_copy(s).wait_recv()
        s_copy(s).start()

    def part_of(s):
        columns = pl.ds(pl.multiple_of(owner(s) * block, 128), block)
        return dot(table[:, columns], xs[s])

    rows = part_of(0)
    for i, s in enumerate(order):
        if i > 0:
            s_arrival(s).wait_recv()
        rows = rows + part_of(s)
    taken[0] = rows.astype(BF16)

    def b_copy(source, dx, dy):
        s = dx * 2 + dy if source == 0 else dx * 2 + 1
        return remote(taken.at[source], taken.at[s], b_send.at[s], b_recv.at[s], to_row(dx, dy))

    def b_arrival(s):
        return remote(taken.at[s], taken.at[s], b_send.at[s], b_recv.at[s], other_y)

    b_out = [b_copy(0, 0, 1), b_copy(0, 2, 0), b_copy(0, 1, 0), b_copy(0, 3, 0)]
    for copy in b_out:
        copy.start()

    for q, dx in ((0, 1), (0, 3), (0, 0), (1, 2), (1, 1)):
        y_start(q, dx)

    def pair_sum(q, dx):
        y_copy(q, dx).wait_recv()
        gate, upper = part(q, dx * 2)
        return gate + yrecv[q, dx, :, :chunk].astype(F32), upper + yrecv[q, dx, :, chunk:].astype(F32)

    def pair_send(q, dx):
        gate, upper = pair_sum(q, dx)
        xsend[q, dx - 1, :, :chunk] = gate.astype(BF16)
        xsend[q, dx - 1, :, chunk:] = upper.astype(BF16)
        x_copy(q, dx).start()

    b_arrival(1).wait_recv()
    relayed = [b_copy(1, dx, 0) for dx in (2, 1, 3)]
    for copy in relayed:
        copy.start()
    b_out += relayed
    for dx in (2, 1, 3):
        pair_send(0, dx)

    for s in (2, 3, 4, 5, 6, 7):
        b_arrival(s).wait_recv()
    loads[3].wait()
    loads[4].wait()

    def score_part(s, total):
        line = router[:, pl.ds(pl.multiple_of(owner(s) * width, 128), width)].astype(F32)
        return total + jnp.sum(taken[s].astype(F32) * line, axis=1, keepdims=True)

    logit = lax.fori_loop(0, ROWS, score_part, jnp.zeros((slots, 1), F32))
    score = 1.0 / (1.0 + jnp.exp(-logit))

    def expert_part(s, sums):
        gate, upper = sums
        scaled = (taken[s].astype(F32) * score).astype(BF16)
        features = pl.ds(pl.multiple_of(owner(s) * width, 128), width)
        return gate + dot(scaled, wg[features, :]), upper + dot(scaled, wu[features, :])

    zero = jnp.zeros((slots, wg.shape[1]), F32)
    gate, upper = lax.fori_loop(0, ROWS, expert_part, (zero, zero))
    hid_e[...] = (silu(gate) * upper).astype(BF16)

    def d_copy(q, s, cross):
        target = to_row(s // 2, s % 2) | ({"core": 1 - core} if cross else {})
        return remote(
            mine_h.at[q, his if cross else mine], hid.at[q, s, :, units],
            d_send.at[q, s, cross], d_recv.at[q, s, cross], target,
        )

    def d_arrival(q, s, cross):
        there = pl.ds(pl.multiple_of((1 - core) * chunk, chunk), chunk) if cross else units
        return remote(mine_h.at[q, mine], hid.at[q, s, :, there], d_send.at[q, s, cross], d_recv.at[q, s, cross], other_y)

    def d_relay(q, dx):
        s = dx * 2 + 1
        return remote(hid.at[q, 1], hid.at[q, s], d_send.at[q, s, 0], d_recv.at[q, s, 0], to_row(dx, 0))

    d_out = []

    def block_end(q):
        gate, upper = pair_sum(q, 0)
        for dx in (2, 1, 3):
            x_copy(q, dx).wait_recv()
            gate = gate + xrecv[q, dx - 1, :, :chunk].astype(F32)
            upper = upper + xrecv[q, dx - 1, :, chunk:].astype(F32)
        mine_h[q] = (silu(gate) * upper).astype(BF16)
        hid[q, 0, :, units] = mine_h[q, mine, :]
        for s in (1, 2, 6, 4, 0):
            for cross in (0, 1):
                if s or cross:
                    copy = d_copy(q, s, cross)
                    copy.start()
                    d_out.append(copy)

    def block_relay(q):
        for cross in (0, 1):
            d_arrival(q, 1, cross).wait_recv()
        for dx in (1, 3, 2):
            copy = d_relay(q, dx)
            copy.start()
            d_out.append(copy)

    block_end(0)
    y_start(1, 3)
    y_start(1, 0)
    pair_send(1, 2)

    def result_part(dx, dy):
        target = ahead(4 - dx) * 2 + lax.rem(yl + dy, 2)
        return dot(hid_e[...], wd[:, pl.ds(pl.multiple_of(target * width, 128), width)])

    def ey_copy(dx):
        return remote(eysend.at[dx], eyrecv.at[dx], ey_send.at[dx], ey_recv.at[dx], other_y)

    def ex_copy(dx):
        return remote(exsend.at[dx - 1], exrecv.at[dx - 1], ex_send.at[dx - 1], ex_recv.at[dx - 1], {"x": ahead(4 - dx)})

    def result_start(dx):
        eysend[dx] = result_part(dx, 1).astype(BF16)
        ey_copy(dx).start()

    def result_sum(dx):
        ey_copy(dx).wait_recv()
        return result_part(dx, 0) + eyrecv[dx].astype(F32)

    loads[5].wait()
    for dx in (2, 1, 3):
        result_start(dx)
    pair_send(1, 1)
    block_relay(0)
    pair_send(1, 3)
    block_end(1)
    result_start(0)
    for dx in (2, 1, 3):
        exsend[dx - 1] = result_sum(dx).astype(BF16)
        ex_copy(dx).start()
    block_relay(1)
    total = result_sum(0)
    for dx in (2, 1, 3):
        ex_copy(dx).wait_recv()
        total = total + exrecv[dx - 1].astype(F32)
    high = total.astype(BF16)
    hilo[:slots] = high
    hilo[slots : 2 * slots] = (total - high.astype(F32)).astype(BF16)
    k_copy = remote(hilo.at[: 2 * slots], hilo.at[2 * slots :], k_send, k_recv, sibling)
    k_copy.start()
    for q in (0, 1):
        loads[6 + q].wait()
        w_out[q].wait_recv()
        d_arrival(q, 0, 1).wait_recv()
    k_copy.wait_recv()

    def f_copy(s, q):
        target = {"yh": lax.rem(yh + q // 4, 2), "z": lax.rem(z + q % 4, 4)}
        return remote(fsend.at[s], frecv.at[q - 1], f_send.at[q - 1], f_recv.at[q - 1], target)

    def finish(s):
        j = owner(s)
        tokens_of = pl.ds(pl.multiple_of(j * block + core * half, half), half)
        total = dot(hid[0, s], sd[0]) + dot(hid[1, s], sd[1]) + dot(place[tokens_of, :], hilo[...])
        q = lax.rem(j // 4 + yh, 2) * 4 + lax.rem(lax.rem(j, 4) + 4 - z, 4)

        @pl.when(q == 0)
        def _():
            own[...] = total

        @pl.when(q > 0)
        def _():
            fsend[s] = total.astype(BF16)
            f_copy(s, q).start()

    for s in (0, 1, 2, 6, 4, 3, 7, 5):
        for q in (0, 1):
            if s in (2, 4, 6):
                d_arrival(q, s, 0).wait_recv()
                d_arrival(q, s, 1).wait_recv()
            elif s > 1:
                d_relay(q, s // 2).wait_recv()
        finish(s)

    total = own[...]
    for q in range(1, ROWS):
        f_copy(0, q).wait_recv()
        total = total + frecv[q - 1].astype(F32)
    out[...] = total.astype(BF16)

    for s in order:
        a_copy(s).wait_send()
        s_copy(s).wait_send()
    for dx in range(4):
        y_copy(0, dx).wait_send()
        y_copy(1, dx).wait_send()
        ey_copy(dx).wait_send()
    for dx in (1, 2, 3):
        x_copy(0, dx).wait_send()
        x_copy(1, dx).wait_send()
        ex_copy(dx).wait_send()
    for copy in b_out + d_out + w_out + [k_copy]:
        copy.wait_send()
    for q in range(1, ROWS):
        f_copy(0, q).wait_send()


def per_device(tokens, expert_ids, modality, tile_counts, router, w_gate, w_up, w_down, shared_gate, shared_up, shared_down):
    block, depth = tokens.shape
    width = shared_down.shape[1]
    hidden = shared_gate.shape[1]
    inner = w_gate.shape[2]
    slots = 2 * MAXT * TILE
    half = block // 2
    chunk = hidden // 2
    count = expert_ids.shape[0]
    vmem = pl.BlockSpec(memory_space=pltpu.VMEM)
    hbm = pl.BlockSpec(memory_space=pl.ANY)
    dma = pltpu.SemaphoreType.DMA
    return pl.pallas_call(
        kernel,
        name="layer",
        out_shape=jax.ShapeDtypeStruct((half, width), BF16),
        in_specs=[vmem, vmem, pl.BlockSpec(memory_space=pltpu.SMEM), hbm, vmem] + [hbm] * 6,
        out_specs=vmem,
        scratch_shapes=[
            pltpu.VMEM((depth, inner), BF16),
            pltpu.VMEM((depth, inner), BF16),
            pltpu.VMEM((inner, depth), BF16),
            pltpu.VMEM((width, hidden), BF16),
            pltpu.VMEM((width, hidden), BF16),
            pltpu.VMEM((2, 2 * chunk, width), BF16),
            pltpu.VMEM((ROWS, block, width), BF16),
            pltpu.VMEM((slots, count), BF16),
            pltpu.VMEM((count, 4 * slots), BF16),
            pltpu.VMEM((2, 4, block, 2 * chunk), BF16),
            pltpu.VMEM((2, 4, block, 2 * chunk), BF16),
            pltpu.VMEM((2, 3, block, 2 * chunk), BF16),
            pltpu.VMEM((2, 3, block, 2 * chunk), BF16),
            pltpu.VMEM((ROWS, slots, width), BF16),
            pltpu.VMEM((slots, inner), BF16),
            pltpu.VMEM((4, slots, width), BF16),
            pltpu.VMEM((4, slots, width), BF16),
            pltpu.VMEM((3, slots, width), BF16),
            pltpu.VMEM((3, slots, width), BF16),
            pltpu.VMEM((4 * slots, width), BF16),
            pltpu.VMEM((2, block, chunk), BF16),
            pltpu.VMEM((2, ROWS, half, 2 * chunk), BF16),
            pltpu.VMEM((half, width), F32),
            pltpu.VMEM((ROWS, half, width), BF16),
            pltpu.VMEM((ROWS - 1, half, width), BF16),
            dma((8,)),
            dma((ROWS,)), dma((ROWS,)), dma((ROWS,)), dma((ROWS,)),
            dma((2, 4)), dma((2, 4)), dma((2, 3)), dma((2, 3)),
            dma((ROWS,)), dma((ROWS,)),
            dma((4,)), dma((4,)), dma((3,)), dma((3,)),
            dma((2, ROWS, 2)), dma((2, ROWS, 2)), dma((2,)), dma((2,)), dma, dma, dma((ROWS - 1,)), dma((ROWS - 1,)),
        ],
        compiler_params=pltpu.CompilerParams(
            collective_id=0, has_side_effects=True, vmem_limit_bytes=60 * 1024 * 1024
        ),
    )(
        expert_ids.reshape(1, count), modality.reshape(1, count), tile_counts, tokens, router.reshape(1, depth),
        w_gate, w_up, w_down, shared_gate, shared_up, shared_down,
    )


def solution(mesh):
    split = Mesh(mesh.devices.reshape(4, 2, 2, 4, 2), ("x", "yl", "yh", "z", "core"))
    placed = (
        P(ROW, None),
        P(),
        P(),
        P(),
        P(None, COL),
        P(COL, None, ROW),
        P(COL, None, ROW),
        P(COL, ROW, None),
        P(ROW, COL),
        P(ROW, COL),
        P(COL, ROW),
    )
    return jax.shard_map(
        per_device, mesh=split, in_specs=placed, out_specs=P(COL, ROW), check_vma=False
    )
```

time: 104 us -> 75.1 us (0.72)
  the two profiles are of different devices: /device:TPU:1 before, /device:TPU:25 now
where the time goes in v3:
time: 75.1 us; the launch traced here: 73.7 us
  Pallas kernels  72.2 us (96%)
  local copies, waits for them, and re-layouts  1.53 us (2%)
    pallas_call x1, Pallas kernels, per_device(): pl.pallas_call(kernel, name='layer', out_shape=jax.ShapeDtypeStruct((half...  72.2 us
    unnamed x1, local copies, waits for them, and re-layouts  1.53 us

profile of v3, /device:TPU:25, one launch (start us, length us, event | category | flops | bytes accessed | tf_op | source)
XLA Modules:
  0.0 73.7 jit_solution(17391470823663452787)
XLA Ops:
  0.0 72.2 %layer.1 = bf16[64,640]{1,0:T(8,128)(2,1)} custom-call(s32[1,1024]{1,0:T(1,128)} %bitcast.4, s32[1,1024]{1,0:T(1,128)} %bitcast.5, s32[2,16]{1,0:T(2,128)} %counts.1, bf16[128,5120]{1,0:T(8,128)(2,1)} %tokens.1, bf16[1,5120]{1,0:T(2,128)(2,1)} %bitcast.3, bf16[1,5120,512]{2,1,0:T(8,128)(2,1)} %w_gate.1, bf16[1,5120,512]{2,1,0:T(8,128)(2,1)} %w_up.1, ...), custom_call_target="tpu_custom_call" | custom-call | tf_op jit(solution)/shard_map/layer/pallas_call | solution.py:386
  72.2 1.5 %copy.13 = bf16[64,640]{1,0:T(8,128)(2,1)} copy(bf16[64,640]{1,0:T(8,128)(2,1)} %layer.1) | data formatting | bytes 163840

commit v4 on v3

--- a/solution.py
+++ b/solution.py
@@ -27,17 +27,21 @@
 def kernel(
     ids, mod, counts, tokens, router, w_gate, w_up, w_down, s_gate, s_up, s_down,
     out,
-    wg, wu, wd, sg, su, sd, xs, table, place, ysend, yrecv, xsend, xrecv, taken,
-    hid_e, eysend, eyrecv, exsend, exrecv, hilo, mine_h, hid, own, fsend, frecv,
+    rows_in, wg, wu, wd, sg, su, sd0, sd1, xs, table, place,
+    ysend0, ysend1, yrecv0, yrecv1, xsend0, xsend1, xrecv0, xrecv1, taken,
+    hid_e, eysend, eyrecv, exsend, exrecv, efar, egot, hilo, mine_h0, mine_h1, hid0, hid1, early, own, fsend, frecv,
     load_sem, a_send, a_recv, s_send, s_recv, y_send, y_recv, x_send, x_recv, b_send, b_recv,
-    ey_send, ey_recv, ex_send, ex_recv, d_send, d_recv, w_send, w_recv, k_send, k_recv, f_send, f_recv,
+    ey_send, ey_recv, ex_send, ex_recv, ef_send, ef_recv, d_send, d_recv, w_send, w_recv, k_send, k_recv, f_send, f_recv,
 ):
     x, yl, yh = lax.axis_index("x"), lax.axis_index("yl"), lax.axis_index("yh")
     z, core = lax.axis_index("z"), lax.axis_index("core")
     block, width = xs.shape[1], xs.shape[2]
     half = block // 2
     slots = table.shape[0]
-    chunk = mine_h.shape[2]
+    sd, mine_h, hid = (sd0, sd1), (mine_h0, mine_h1), (hid0, hid1)
+    ysend, yrecv, xsend, xrecv = (ysend0, ysend1), (yrecv0, yrecv1), (xsend0, xsend1), (xrecv0, xrecv1)
+    sizes = (mine_h0.shape[1], mine_h1.shape[1])
+    spans = (slice(0, sizes[0]), slice(sizes[0], sizes[0] + sizes[1]))
     row = x * 2 + yl
     expert = yh * 8 + z * 2 + core
 
@@ -59,17 +63,19 @@
             src_ref=src, dst_ref=dst, send_sem=send, recv_sem=recv, device_id=device, device_id_type=MESH
         )
 
-    units = pl.ds(pl.multiple_of(core * chunk, chunk), chunk)
+    def units(q, of):
+        return pl.ds(pl.multiple_of(of * sizes[q], 128), sizes[q])
 
     loads = [
-        pltpu.make_async_copy(tokens.at[:, pl.ds(pl.multiple_of(row * width, 128), width)], xs.at[0], load_sem.at[0]),
+        pltpu.make_async_copy(tokens, rows_in, load_sem.at[0]),
+        pltpu.make_async_copy(tokens.at[:, pl.ds(pl.multiple_of(row * width, 128), width)], xs.at[0], load_sem.at[9]),
         pltpu.make_async_copy(s_gate, sg, load_sem.at[1]),
         pltpu.make_async_copy(s_up, su, load_sem.at[2]),
         pltpu.make_async_copy(w_gate.at[0], wg, load_sem.at[3]),
         pltpu.make_async_copy(w_up.at[0], wu, load_sem.at[4]),
         pltpu.make_async_copy(w_down.at[0], wd, load_sem.at[5]),
-        pltpu.make_async_copy(s_down.at[:chunk], sd.at[0, units], load_sem.at[6]),
-        pltpu.make_async_copy(s_down.at[chunk:], sd.at[1, units], load_sem.at[7]),
+        pltpu.make_async_copy(s_down.at[spans[0]], sd[0].at[units(0, core)], load_sem.at[6]),
+        pltpu.make_async_copy(s_down.at[spans[1]], sd[1].at[units(1, core)], load_sem.at[7]),
     ]
     for load in loads:
         load.start()
@@ -111,7 +117,7 @@
         dx, dy = s // 2, s % 2
         target = ahead(dx) * 2 + lax.rem(yl + dy, 2)
         return remote(
-            tokens.at[mine, pl.ds(pl.multiple_of(target * width, 128), width)],
+            rows_in.at[mine, pl.ds(pl.multiple_of(target * width, 128), width)],
             xs.at[s, mine], a_send.at[s], a_recv.at[s], to_row(dx, dy),
         )
 
@@ -122,20 +128,20 @@
         return remote(xs.at[s, his], xs.at[s, his], s_send.at[s], s_recv.at[s], sibling)
 
     order = (5, 3, 7, 1, 4, 2, 6)
+    loads[0].wait()
     for s in order:
         a_copy(s).start()
-    loads[0].wait()
 
     def y_copy(q, dx):
-        return remote(ysend.at[q, dx], yrecv.at[q, dx], y_send.at[q, dx], y_recv.at[q, dx], other_y)
+        return remote(ysend[q].at[dx], yrecv[q].at[dx], y_send.at[q, dx], y_recv.at[q, dx], other_y)
 
     def x_copy(q, dx):
         return remote(
-            xsend.at[q, dx - 1], xrecv.at[q, dx - 1], x_send.at[q, dx - 1], x_recv.at[q, dx - 1], {"x": ahead(4 - dx)}
+            xsend[q].at[dx - 1], xrecv[q].at[dx - 1], x_send.at[q, dx - 1], x_recv.at[q, dx - 1], {"x": ahead(4 - dx)}
         )
 
     w_out = [
-        remote(s_down.at[q * chunk : (q + 1) * chunk], sd.at[q, units], w_send.at[q], w_recv.at[q], sibling)
+        remote(s_down.at[spans[q]], sd[q].at[units(q, core)], w_send.at[q], w_recv.at[q], sibling)
         for q in (0, 1)
     ]
     for copy in w_out:
@@ -144,17 +150,16 @@
     place[:, 2 * slots :] = jnp.concatenate([ones, ones], axis=0).T.astype(BF16)
 
     def part(q, s):
-        columns = slice(q * chunk, (q + 1) * chunk)
-        return dot(xs[s], sg[:, columns]), dot(xs[s], su[:, columns])
+        return dot(xs[s], sg[:, spans[q]]), dot(xs[s], su[:, spans[q]])
 
     def y_start(q, dx):
         gate, upper = part(q, dx * 2 + 1)
-        ysend[q, dx, :, :chunk] = gate.astype(BF16)
-        ysend[q, dx, :, chunk:] = upper.astype(BF16)
+        ysend[q][dx, :, : sizes[q]] = gate.astype(BF16)
+        ysend[q][dx, :, sizes[q] :] = upper.astype(BF16)
         y_copy(q, dx).start()
 
-    loads[1].wait()
-    loads[2].wait()
+    for load in loads[1:4]:
+        load.wait()
     for s in order[:2]:
         a_copy(s).wait_recv()
         s_copy(s).start()
@@ -186,18 +191,18 @@
     for copy in b_out:
         copy.start()
 
-    for q, dx in ((0, 1), (0, 3), (0, 0), (1, 2), (1, 1)):
+    for q, dx in ((0, 1), (0, 3), (0, 0), (1, 2), (1, 1), (1, 3)):
         y_start(q, dx)
 
     def pair_sum(q, dx):
         y_copy(q, dx).wait_recv()
         gate, upper = part(q, dx * 2)
-        return gate + yrecv[q, dx, :, :chunk].astype(F32), upper + yrecv[q, dx, :, chunk:].astype(F32)
+        return gate + yrecv[q][dx, :, : sizes[q]].astype(F32), upper + yrecv[q][dx, :, sizes[q] :].astype(F32)
 
     def pair_send(q, dx):
         gate, upper = pair_sum(q, dx)
-        xsend[q, dx - 1, :, :chunk] = gate.astype(BF16)
-        xsend[q, dx - 1, :, chunk:] = upper.astype(BF16)
+        xsend[q][dx - 1, :, : sizes[q]] = gate.astype(BF16)
+        xsend[q][dx - 1, :, sizes[q] :] = upper.astype(BF16)
         x_copy(q, dx).start()
 
     b_arrival(1).wait_recv()
@@ -210,8 +215,8 @@
 
     for s in (2, 3, 4, 5, 6, 7):
         b_arrival(s).wait_recv()
-    loads[3].wait()
     loads[4].wait()
+    loads[5].wait()
 
     def score_part(s, total):
         line = router[:, pl.ds(pl.multiple_of(owner(s) * width, 128), width)].astype(F32)
@@ -233,17 +238,17 @@
     def d_copy(q, s, cross):
         target = to_row(s // 2, s % 2) | ({"core": 1 - core} if cross else {})
         return remote(
-            mine_h.at[q, his if cross else mine], hid.at[q, s, :, units],
+            mine_h[q].at[his if cross else mine], hid[q].at[s, :, units(q, core)],
             d_send.at[q, s, cross], d_recv.at[q, s, cross], target,
         )
 
     def d_arrival(q, s, cross):
-        there = pl.ds(pl.multiple_of((1 - core) * chunk, chunk), chunk) if cross else units
-        return remote(mine_h.at[q, mine], hid.at[q, s, :, there], d_send.at[q, s, cross], d_recv.at[q, s, cross], other_y)
+        there = units(q, 1 - core if cross else core)
+        return remote(mine_h[q].at[mine], hid[q].at[s, :, there], d_send.at[q, s, cross], d_recv.at[q, s, cross], other_y)
 
     def d_relay(q, dx):
         s = dx * 2 + 1
-        return remote(hid.at[q, 1], hid.at[q, s], d_send.at[q, s, 0], d_recv.at[q, s, 0], to_row(dx, 0))
+        return remote(hid[q].at[1], hid[q].at[s], d_send.at[q, s, 0], d_recv.at[q, s, 0], to_row(dx, 0))
 
     d_out = []
 
@@ -251,10 +256,10 @@
         gate, upper = pair_sum(q, 0)
         for dx in (2, 1, 3):
             x_copy(q, dx).wait_recv()
-            gate = gate + xrecv[q, dx - 1, :, :chunk].astype(F32)
-            upper = upper + xrecv[q, dx - 1, :, chunk:].astype(F32)
-        mine_h[q] = (silu(gate) * upper).astype(BF16)
-        hid[q, 0, :, units] = mine_h[q, mine, :]
+            gate = gate + xrecv[q][dx - 1, :, : sizes[q]].astype(F32)
+            upper = upper + xrecv[q][dx - 1, :, sizes[q] :].astype(F32)
+        mine_h[q][...] = (silu(gate) * upper).astype(BF16)
+        hid[q][0, :, units(q, core)] = mine_h[q][mine, :]
         for s in (1, 2, 6, 4, 0):
             for cross in (0, 1):
                 if s or cross:
@@ -270,11 +275,6 @@
             copy.start()
             d_out.append(copy)
 
-    block_end(0)
-    y_start(1, 3)
-    y_start(1, 0)
-    pair_send(1, 2)
-
     def result_part(dx, dy):
         target = ahead(4 - dx) * 2 + lax.rem(yl + dy, 2)
         return dot(hid_e[...], wd[:, pl.ds(pl.multiple_of(target * width, 128), width)])
@@ -283,51 +283,57 @@
         return remote(eysend.at[dx], eyrecv.at[dx], ey_send.at[dx], ey_recv.at[dx], other_y)
 
     def ex_copy(dx):
-        return remote(exsend.at[dx - 1], exrecv.at[dx - 1], ex_send.at[dx - 1], ex_recv.at[dx - 1], {"x": ahead(4 - dx)})
-
-    def result_start(dx):
+        return remote(exsend.at[dx], exrecv.at[dx], ex_send.at[dx], ex_recv.at[dx], {"x": ahead(4 - dx)})
+
+    far_copy = remote(efar, egot, ef_send, ef_recv, {"x": ahead(2)})
+
+    loads[6].wait()
+    efar[0] = result_part(2, 0).astype(BF16)
+    efar[1] = result_part(2, 1).astype(BF16)
+    far_copy.start()
+    for dx in (1, 3):
         eysend[dx] = result_part(dx, 1).astype(BF16)
         ey_copy(dx).start()
-
-    def result_sum(dx):
+    y_start(1, 0)
+    for dx in (2, 1, 3):
+        pair_send(1, dx)
+    far_copy.wait_recv()
+    eysend[0] = (result_part(0, 1) + egot[1].astype(F32)).astype(BF16)
+    ey_copy(0).start()
+    for dx in (1, 3):
         ey_copy(dx).wait_recv()
-        return result_part(dx, 0) + eyrecv[dx].astype(F32)
-
-    loads[5].wait()
-    for dx in (2, 1, 3):
-        result_start(dx)
-    pair_send(1, 1)
+        exsend[dx] = (result_part(dx, 0) + eyrecv[dx].astype(F32)).astype(BF16)
+        ex_copy(dx).start()
+    block_end(0)
+    total = result_part(0, 0) + egot[0].astype(F32)
+    block_end(1)
     block_relay(0)
-    pair_send(1, 3)
-    block_end(1)
-    result_start(0)
-    for dx in (2, 1, 3):
-        exsend[dx - 1] = result_sum(dx).astype(BF16)
-        ex_copy(dx).start()
-    block_relay(1)
-    total = result_sum(0)
-    for dx in (2, 1, 3):
+    ey_copy(0).wait_recv()
+    total = total + eyrecv[0].astype(F32)
+    for dx in (1, 3):
         ex_copy(dx).wait_recv()
-        total = total + exrecv[dx - 1].astype(F32)
+        total = total + exrecv[dx].astype(F32)
     high = total.astype(BF16)
     hilo[:slots] = high
     hilo[slots : 2 * slots] = (total - high.astype(F32)).astype(BF16)
     k_copy = remote(hilo.at[: 2 * slots], hilo.at[2 * slots :], k_send, k_recv, sibling)
     k_copy.start()
     for q in (0, 1):
-        loads[6 + q].wait()
+        loads[7 + q].wait()
         w_out[q].wait_recv()
         d_arrival(q, 0, 1).wait_recv()
-    k_copy.wait_recv()
 
     def f_copy(s, q):
         target = {"yh": lax.rem(yh + q // 4, 2), "z": lax.rem(z + q % 4, 4)}
         return remote(fsend.at[s], frecv.at[q - 1], f_send.at[q - 1], f_recv.at[q - 1], target)
 
-    def finish(s):
+    def begin(s):
+        tokens_of = pl.ds(pl.multiple_of(owner(s) * block + core * half, half), half)
+        return dot(hid[0][s], sd[0][...]) + dot(place[tokens_of, :], hilo[...])
+
+    def finish(s, begun=None):
         j = owner(s)
-        tokens_of = pl.ds(pl.multiple_of(j * block + core * half, half), half)
-        total = dot(hid[0, s], sd[0]) + dot(hid[1, s], sd[1]) + dot(place[tokens_of, :], hilo[...])
+        total = (begin(s) if begun is None else begun) + dot(hid[1][s], sd[1][...])
         q = lax.rem(j // 4 + yh, 2) * 4 + lax.rem(lax.rem(j, 4) + 4 - z, 4)
 
         @pl.when(q == 0)
@@ -339,14 +345,24 @@
             fsend[s] = total.astype(BF16)
             f_copy(s, q).start()
 
-    for s in (0, 1, 2, 6, 4, 3, 7, 5):
+    def arrive(s):
         for q in (0, 1):
-            if s in (2, 4, 6):
-                d_arrival(q, s, 0).wait_recv()
-                d_arrival(q, s, 1).wait_recv()
-            elif s > 1:
-                d_relay(q, s // 2).wait_recv()
+            d_arrival(q, s, 0).wait_recv()
+            d_arrival(q, s, 1).wait_recv()
+
+    block_relay(1)
+    k_copy.wait_recv()
+    finish(0)
+    finish(1)
+    for s in (2, 6, 4):
+        arrive(s)
         finish(s)
+    for dx in (1, 3, 2):
+        d_relay(0, dx).wait_recv()
+        early[dx - 1] = begin(dx * 2 + 1)
+    for dx in (1, 3, 2):
+        d_relay(1, dx).wait_recv()
+        finish(dx * 2 + 1, early[dx - 1])
 
     total = own[...]
     for q in range(1, ROWS):
@@ -360,12 +376,11 @@
     for dx in range(4):
         y_copy(0, dx).wait_send()
         y_copy(1, dx).wait_send()
-        ey_copy(dx).wait_send()
     for dx in (1, 2, 3):
         x_copy(0, dx).wait_send()
         x_copy(1, dx).wait_send()
-        ex_copy(dx).wait_send()
-    for copy in b_out + d_out + w_out + [k_copy]:
+    e_out = [ey_copy(0), ey_copy(1), ey_copy(3), ex_copy(1), ex_copy(3), far_copy]
+    for copy in b_out + d_out + e_out + w_out + [k_copy]:
         copy.wait_send()
     for q in range(1, ROWS):
         f_copy(0, q).wait_send()
@@ -378,7 +393,7 @@
     inner = w_gate.shape[2]
     slots = 2 * MAXT * TILE
     half = block // 2
-    chunk = hidden // 2
+    sizes = (256, hidden - 256)
     count = expert_ids.shape[0]
     vmem = pl.BlockSpec(memory_space=pltpu.VMEM)
     hbm = pl.BlockSpec(memory_space=pl.ANY)
@@ -390,36 +405,38 @@
         in_specs=[vmem, vmem, pl.BlockSpec(memory_space=pltpu.SMEM), hbm, vmem] + [hbm] * 6,
         out_specs=vmem,
         scratch_shapes=[
+            pltpu.VMEM((block, depth), BF16),
             pltpu.VMEM((depth, inner), BF16),
             pltpu.VMEM((depth, inner), BF16),
             pltpu.VMEM((inner, depth), BF16),
             pltpu.VMEM((width, hidden), BF16),
             pltpu.VMEM((width, hidden), BF16),
-            pltpu.VMEM((2, 2 * chunk, width), BF16),
+            *(pltpu.VMEM((2 * size, width), BF16) for size in sizes),
             pltpu.VMEM((ROWS, block, width), BF16),
             pltpu.VMEM((slots, count), BF16),
             pltpu.VMEM((count, 4 * slots), BF16),
-            pltpu.VMEM((2, 4, block, 2 * chunk), BF16),
-            pltpu.VMEM((2, 4, block, 2 * chunk), BF16),
-            pltpu.VMEM((2, 3, block, 2 * chunk), BF16),
-            pltpu.VMEM((2, 3, block, 2 * chunk), BF16),
+            *(pltpu.VMEM((4, block, 2 * size), BF16) for size in sizes + sizes),
+            *(pltpu.VMEM((3, block, 2 * size), BF16) for size in sizes + sizes),
             pltpu.VMEM((ROWS, slots, width), BF16),
             pltpu.VMEM((slots, inner), BF16),
             pltpu.VMEM((4, slots, width), BF16),
             pltpu.VMEM((4, slots, width), BF16),
-            pltpu.VMEM((3, slots, width), BF16),
-            pltpu.VMEM((3, slots, width), BF16),
+            pltpu.VMEM((4, slots, width), BF16),
+            pltpu.VMEM((4, slots, width), BF16),
+            pltpu.VMEM((2, slots, width), BF16),
+            pltpu.VMEM((2, slots, width), BF16),
             pltpu.VMEM((4 * slots, width), BF16),
-            pltpu.VMEM((2, block, chunk), BF16),
-            pltpu.VMEM((2, ROWS, half, 2 * chunk), BF16),
+            *(pltpu.VMEM((block, size), BF16) for size in sizes),
+            *(pltpu.VMEM((ROWS, half, 2 * size), BF16) for size in sizes),
+            pltpu.VMEM((3, half, width), F32),
             pltpu.VMEM((half, width), F32),
             pltpu.VMEM((ROWS, half, width), BF16),
             pltpu.VMEM((ROWS - 1, half, width), BF16),
-            dma((8,)),
+            dma((10,)),
             dma((ROWS,)), dma((ROWS,)), dma((ROWS,)), dma((ROWS,)),
             dma((2, 4)), dma((2, 4)), dma((2, 3)), dma((2, 3)),
             dma((ROWS,)), dma((ROWS,)),
-            dma((4,)), dma((4,)), dma((3,)), dma((3,)),
+            dma((4,)), dma((4,)), dma((4,)), dma((4,)), dma, dma,
             dma((2, ROWS, 2)), dma((2, ROWS, 2)), dma((2,)), dma((2,)), dma, dma, dma((ROWS - 1,)), dma((ROWS - 1,)),
         ],
         compiler_params=pltpu.CompilerParams(

time: 75.1 us -> 70.9 us (0.944); the launches traced: 73.7 us -> 70.7 us
  Pallas kernels: 72.2 us -> 69.2 us
    pallas_call x1, Pallas kernels: 72.2 us -> 69.2 us  [per_device(): pl.pallas_call(kernel, name='layer', out_shape=jax.ShapeDtypeStruct((half...]
where the time goes in v4:
time: 70.9 us; the launch traced here: 70.7 us
  Pallas kernels  69.2 us (98%)
  local copies, waits for them, and re-layouts  1.53 us (2%)
    pallas_call x1, Pallas kernels, per_device(): pl.pallas_call(kernel, name='layer', out_shape=jax.ShapeDtypeStruct((half...  69.2 us
    unnamed x1, local copies, waits for them, and re-layouts  1.53 us

profile of v4, /device:TPU:25, one launch (start us, length us, event | category | flops | bytes accessed | tf_op | source)
XLA Modules:
  0.0 70.7 jit_solution(12256719579073447053)
XLA Ops:
  0.0 69.2 %layer.1 = bf16[64,640]{1,0:T(8,128)(2,1)} custom-call(s32[1,1024]{1,0:T(1,128)} %bitcast.4, s32[1,1024]{1,0:T(1,128)} %bitcast.5, s32[2,16]{1,0:T(2,128)} %counts.1, bf16[128,5120]{1,0:T(8,128)(2,1)} %tokens.1, bf16[1,5120]{1,0:T(2,128)(2,1)} %bitcast.3, bf16[1,5120,512]{2,1,0:T(8,128)(2,1)} %w_gate.1, bf16[1,5120,512]{2,1,0:T(8,128)(2,1)} %w_up.1, ...), custom_call_target="tpu_custom_call" | custom-call | tf_op jit(solution)/shard_map/layer/pallas_call | solution.py:401
  69.2 1.5 %copy.13 = bf16[64,640]{1,0:T(8,128)(2,1)} copy(bf16[64,640]{1,0:T(8,128)(2,1)} %layer.1) | data formatting | bytes 163840

commit v5 on v4

--- a/solution.py
+++ b/solution.py
@@ -104,10 +104,6 @@
         spot = jnp.where(member & (rank < limit), kind * (MAXT * TILE) + rank, -1)
         return (at == jnp.maximum(spot[0:1, :], spot[1:2, :])).astype(F32)
 
-    ones = ones_of(expert)
-    table[...] = ones.astype(BF16)
-    place[:, : 2 * slots] = jnp.concatenate([ones, ones], axis=0).T.astype(BF16)
-
     pl.semaphore_wait(barrier, len(peers))
 
     mine = pl.ds(pl.multiple_of(core * half, half), half)
@@ -118,14 +114,14 @@
         target = ahead(dx) * 2 + lax.rem(yl + dy, 2)
         return remote(
             rows_in.at[mine, pl.ds(pl.multiple_of(target * width, 128), width)],
-            xs.at[s, mine], a_send.at[s], a_recv.at[s], to_row(dx, dy),
+            xs.at[s, mine], a_send, a_recv.at[s], to_row(dx, dy),
         )
 
     def s_copy(s):
-        return remote(xs.at[s, mine], xs.at[s, mine], s_send.at[s], s_recv.at[s], sibling)
+        return remote(xs.at[s, mine], xs.at[s, mine], s_send, s_recv.at[s], sibling)
 
     def s_arrival(s):
-        return remote(xs.at[s, his], xs.at[s, his], s_send.at[s], s_recv.at[s], sibling)
+        return remote(xs.at[s, his], xs.at[s, his], s_send, s_recv.at[s], sibling)
 
     order = (5, 3, 7, 1, 4, 2, 6)
     loads[0].wait()
@@ -133,11 +129,11 @@
         a_copy(s).start()
 
     def y_copy(q, dx):
-        return remote(ysend[q].at[dx], yrecv[q].at[dx], y_send.at[q, dx], y_recv.at[q, dx], other_y)
+        return remote(ysend[q].at[dx], yrecv[q].at[dx], y_send.at[q], y_recv.at[q, dx], other_y)
 
     def x_copy(q, dx):
         return remote(
-            xsend[q].at[dx - 1], xrecv[q].at[dx - 1], x_send.at[q, dx - 1], x_recv.at[q, dx - 1], {"x": ahead(4 - dx)}
+            xsend[q].at[dx - 1], xrecv[q].at[dx - 1], x_send.at[q], x_recv.at[q, dx - 1], {"x": ahead(4 - dx)}
         )
 
     w_out = [
@@ -146,6 +142,9 @@
     ]
     for copy in w_out:
         copy.start()
+    ones = ones_of(expert)
+    table[...] = ones.astype(BF16)
+    place[:, : 2 * slots] = jnp.concatenate([ones, ones], axis=0).T.astype(BF16)
     ones = ones_of(yh * 8 + z * 2 + 1 - core)
     place[:, 2 * slots :] = jnp.concatenate([ones, ones], axis=0).T.astype(BF16)
 
@@ -182,10 +181,10 @@
 
     def b_copy(source, dx, dy):
         s = dx * 2 + dy if source == 0 else dx * 2 + 1
-        return remote(taken.at[source], taken.at[s], b_send.at[s], b_recv.at[s], to_row(dx, dy))
+        return remote(taken.at[source], taken.at[s], b_send, b_recv.at[s], to_row(dx, dy))
 
     def b_arrival(s):
-        return remote(taken.at[s], taken.at[s], b_send.at[s], b_recv.at[s], other_y)
+        return remote(taken.at[s], taken.at[s], b_send, b_recv.at[s], other_y)
 
     b_out = [b_copy(0, 0, 1), b_copy(0, 2, 0), b_copy(0, 1, 0), b_copy(0, 3, 0)]
     for copy in b_out:
@@ -239,18 +238,16 @@
         target = to_row(s // 2, s % 2) | ({"core": 1 - core} if cross else {})
         return remote(
             mine_h[q].at[his if cross else mine], hid[q].at[s, :, units(q, core)],
-            d_send.at[q, s, cross], d_recv.at[q, s, cross], target,
+            d_send.at[q], d_recv.at[q, s, cross], target,
         )
 
     def d_arrival(q, s, cross):
         there = units(q, 1 - core if cross else core)
-        return remote(mine_h[q].at[mine], hid[q].at[s, :, there], d_send.at[q, s, cross], d_recv.at[q, s, cross], other_y)
+        return remote(mine_h[q].at[mine], hid[q].at[s, :, there], d_send.at[q], d_recv.at[q, s, cross], other_y)
 
     def d_relay(q, dx):
         s = dx * 2 + 1
-        return remote(hid[q].at[1], hid[q].at[s], d_send.at[q, s, 0], d_recv.at[q, s, 0], to_row(dx, 0))
-
-    d_out = []
+        return remote(hid[q].at[1], hid[q].at[s], d_send.at[q], d_recv.at[q, s, 0], to_row(dx, 0))
 
     def block_end(q):
         gate, upper = pair_sum(q, 0)
@@ -265,25 +262,30 @@
                 if s or cross:
                     copy = d_copy(q, s, cross)
                     copy.start()
-                    d_out.append(copy)
-
-    def block_relay(q):
+
+    def block_relay(q, steps):
         for cross in (0, 1):
             d_arrival(q, 1, cross).wait_recv()
-        for dx in (1, 3, 2):
+        for dx in steps:
             copy = d_relay(q, dx)
             copy.start()
-            d_out.append(copy)
+
+    def block_across(q, dx):
+        s = dx * 2
+        for cross in (0, 1):
+            d_arrival(q, s, cross).wait_recv()
+        copy = remote(hid[q].at[s], hid[q].at[s + 1], d_send.at[q], d_recv.at[q, s + 1, 0], other_y)
+        copy.start()
 
     def result_part(dx, dy):
         target = ahead(4 - dx) * 2 + lax.rem(yl + dy, 2)
         return dot(hid_e[...], wd[:, pl.ds(pl.multiple_of(target * width, 128), width)])
 
     def ey_copy(dx):
-        return remote(eysend.at[dx], eyrecv.at[dx], ey_send.at[dx], ey_recv.at[dx], other_y)
+        return remote(eysend.at[dx], eyrecv.at[dx], ey_send, ey_recv.at[dx], other_y)
 
     def ex_copy(dx):
-        return remote(exsend.at[dx], exrecv.at[dx], ex_send.at[dx], ex_recv.at[dx], {"x": ahead(4 - dx)})
+        return remote(exsend.at[dx], exrecv.at[dx], ex_send, ex_recv.at[dx], {"x": ahead(4 - dx)})
 
     far_copy = remote(efar, egot, ef_send, ef_recv, {"x": ahead(2)})
 
@@ -307,7 +309,7 @@
     block_end(0)
     total = result_part(0, 0) + egot[0].astype(F32)
     block_end(1)
-    block_relay(0)
+    block_relay(0, (2,))
     ey_copy(0).wait_recv()
     total = total + eyrecv[0].astype(F32)
     for dx in (1, 3):
@@ -325,7 +327,7 @@
 
     def f_copy(s, q):
         target = {"yh": lax.rem(yh + q // 4, 2), "z": lax.rem(z + q % 4, 4)}
-        return remote(fsend.at[s], frecv.at[q - 1], f_send.at[q - 1], f_recv.at[q - 1], target)
+        return remote(fsend.at[s], frecv.at[q - 1], f_send, f_recv.at[q - 1], target)
 
     def begin(s):
         tokens_of = pl.ds(pl.multiple_of(owner(s) * block + core * half, half), half)
@@ -347,10 +349,13 @@
 
     def arrive(s):
         for q in (0, 1):
-            d_arrival(q, s, 0).wait_recv()
-            d_arrival(q, s, 1).wait_recv()
-
-    block_relay(1)
+            if q == 1 or s == 4:
+                d_arrival(q, s, 0).wait_recv()
+                d_arrival(q, s, 1).wait_recv()
+
+    for dx in (1, 3):
+        block_across(0, dx)
+    block_relay(1, (1, 3, 2))
     k_copy.wait_recv()
     finish(0)
     finish(1)
@@ -370,20 +375,22 @@
         total = total + frecv[q - 1].astype(F32)
     out[...] = total.astype(BF16)
 
-    for s in order:
-        a_copy(s).wait_send()
-        s_copy(s).wait_send()
-    for dx in range(4):
-        y_copy(0, dx).wait_send()
-        y_copy(1, dx).wait_send()
-    for dx in (1, 2, 3):
-        x_copy(0, dx).wait_send()
-        x_copy(1, dx).wait_send()
-    e_out = [ey_copy(0), ey_copy(1), ey_copy(3), ex_copy(1), ex_copy(3), far_copy]
-    for copy in b_out + d_out + e_out + w_out + [k_copy]:
-        copy.wait_send()
-    for q in range(1, ROWS):
-        f_copy(0, q).wait_send()
+    def left(bytes_of, sem):
+        pltpu.make_async_copy(bytes_of, bytes_of, sem).wait()
+
+    left(frecv, a_send)
+    left(frecv, s_send)
+    left(frecv, b_send)
+    for q in (0, 1):
+        left(ysend[q], y_send.at[q])
+        left(xsend[q], x_send.at[q])
+        left(xs.at[:3, :, : 5 * sizes[q] // 2], d_send.at[q])
+        w_out[q].wait_send()
+    left(eysend.at[:3], ey_send)
+    left(eysend.at[:2], ex_send)
+    far_copy.wait_send()
+    k_copy.wait_send()
+    left(frecv, f_send)
 
 
 def per_device(tokens, expert_ids, modality, tile_counts, router, w_gate, w_up, w_down, shared_gate, shared_up, shared_down):
@@ -401,7 +408,7 @@
     return pl.pallas_call(
         kernel,
         name="layer",
-        out_shape=jax.ShapeDtypeStruct((half, width), BF16),
+        out_shape=pltpu.VMEM((half, width), BF16),
         in_specs=[vmem, vmem, pl.BlockSpec(memory_space=pltpu.SMEM), hbm, vmem] + [hbm] * 6,
         out_specs=vmem,
         scratch_shapes=[
@@ -433,11 +440,11 @@
             pltpu.VMEM((ROWS, half, width), BF16),
             pltpu.VMEM((ROWS - 1, half, width), BF16),
             dma((10,)),
-            dma((ROWS,)), dma((ROWS,)), dma((ROWS,)), dma((ROWS,)),
-            dma((2, 4)), dma((2, 4)), dma((2, 3)), dma((2, 3)),
-            dma((ROWS,)), dma((ROWS,)),
-            dma((4,)), dma((4,)), dma((4,)), dma((4,)), dma, dma,
-            dma((2, ROWS, 2)), dma((2, ROWS, 2)), dma((2,)), dma((2,)), dma, dma, dma((ROWS - 1,)), dma((ROWS - 1,)),
+            dma, dma((ROWS,)), dma, dma((ROWS,)),
+            dma((2,)), dma((2, 4)), dma((2,)), dma((2, 3)),
+            dma, dma((ROWS,)),
+            dma, dma((4,)), dma, dma((4,)), dma, dma,
+            dma((2,)), dma((2, ROWS, 2)), dma((2,)), dma((2,)), dma, dma, dma, dma((ROWS - 1,)),
         ],
         compiler_params=pltpu.CompilerParams(
             collective_id=0, has_side_effects=True, vmem_limit_bytes=60 * 1024 * 1024

time: 70.9 us -> 67.9 us (0.958)
  Pallas kernels: 69.2 us -> 67.1 us
  local copies, waits for them, and re-layouts: 1.53 us -> 0.64 us
    pallas_call x1, Pallas kernels: 69.2 us -> 67.1 us  [per_device(): pl.pallas_call(kernel, name='layer', out_shape=pltpu.VMEM((half, width),...]
    unnamed x1, local copies, waits for them, and re-layouts: 1.53 us -> 0.64 us
where the time goes in v5:
time: 67.9 us; the launch traced here: 67.8 us
  Pallas kernels  67.1 us (99%)
    pallas_call x1, Pallas kernels, per_device(): pl.pallas_call(kernel, name='layer', out_shape=pltpu.VMEM((half, width),...  67.1 us

profile of v5, /device:TPU:25, one launch (start us, length us, event | category | flops | bytes accessed | tf_op | source)
XLA Modules:
  0.0 67.8 jit_solution(12201137301001228453)
XLA Ops:
  0.0 67.1 %layer.1 = bf16[64,640]{1,0:T(8,128)(2,1)S(1)} custom-call(s32[1,1024]{1,0:T(1,128)} %bitcast.4, s32[1,1024]{1,0:T(1,128)} %bitcast.5, s32[2,16]{1,0:T(2,128)} %counts.1, bf16[128,5120]{1,0:T(8,128)(2,1)} %tokens.1, bf16[1,5120]{1,0:T(2,128)(2,1)} %bitcast.3, bf16[1,5120,512]{2,1,0:T(8,128)(2,1)} %w_gate.1, bf16[1,5120,512]{2,1,0:T(8,128)(2,1)} %w_up.1, ...), custom_call_target="tpu_custom_call" | custom-call | tf_op jit(solution)/shard_map/layer/pallas_call | solution.py:408
  67.1 0.6 copy.13

commit v6 on v5

--- a/solution.py
+++ b/solution.py
@@ -257,7 +257,7 @@
             upper = upper + xrecv[q][dx - 1, :, sizes[q] :].astype(F32)
         mine_h[q][...] = (silu(gate) * upper).astype(BF16)
         hid[q][0, :, units(q, core)] = mine_h[q][mine, :]
-        for s in (1, 2, 6, 4, 0):
+        for s in (1, 2, 6, 0) if q == 0 else (1, 2, 6, 4, 0):
             for cross in (0, 1):
                 if s or cross:
                     copy = d_copy(q, s, cross)
@@ -270,10 +270,17 @@
             copy = d_relay(q, dx)
             copy.start()
 
+    def d_onward(q, dx):
+        rows = pl.ds(0 if dx == 1 else half // 2, half // 2)
+        return remote(
+            hid[q].at[dx * 2, rows], hid[q].at[4, rows], d_send.at[q], d_recv.at[q, 4, dx // 2], {"x": ahead(dx)}
+        )
+
     def block_across(q, dx):
         s = dx * 2
         for cross in (0, 1):
             d_arrival(q, s, cross).wait_recv()
+        d_onward(q, dx).start()
         copy = remote(hid[q].at[s], hid[q].at[s + 1], d_send.at[q], d_recv.at[q, s + 1, 0], other_y)
         copy.start()
 
@@ -347,24 +354,29 @@
             fsend[s] = total.astype(BF16)
             f_copy(s, q).start()
 
-    def arrive(s):
-        for q in (0, 1):
-            if q == 1 or s == 4:
-                d_arrival(q, s, 0).wait_recv()
-                d_arrival(q, s, 1).wait_recv()
-
     for dx in (1, 3):
         block_across(0, dx)
     block_relay(1, (1, 3, 2))
     k_copy.wait_recv()
     finish(0)
     finish(1)
-    for s in (2, 6, 4):
-        arrive(s)
+    def end_direct(s):
+        d_arrival(1, s, 0).wait_recv()
+        d_arrival(1, s, 1).wait_recv()
         finish(s)
-    for dx in (1, 3, 2):
+
+    def begin_far(dx):
         d_relay(0, dx).wait_recv()
         early[dx - 1] = begin(dx * 2 + 1)
+
+    end_direct(2)
+    end_direct(6)
+    begin_far(1)
+    begin_far(3)
+    d_onward(0, 1).wait_recv()
+    d_onward(0, 3).wait_recv()
+    end_direct(4)
+    begin_far(2)
     for dx in (1, 3, 2):
         d_relay(1, dx).wait_recv()
         finish(dx * 2 + 1, early[dx - 1])

time: 67.9 us -> 66.7 us (0.982)
  Pallas kernels: 67.1 us -> 65.9 us
    pallas_call x1, Pallas kernels: 67.1 us -> 65.9 us  [per_device(): pl.pallas_call(kernel, name='layer', out_shape=pltpu.VMEM((half, width),...]
where the time goes in v6:
time: 66.7 us; the launch traced here: 66.5 us
  Pallas kernels  65.9 us (99%)
    pallas_call x1, Pallas kernels, per_device(): pl.pallas_call(kernel, name='layer', out_shape=pltpu.VMEM((half, width),...  65.9 us

profile of v6, /device:TPU:25, one launch (start us, length us, event | category | flops | bytes accessed | tf_op | source)
XLA Modules:
  0.0 66.5 jit_solution(4891220220859667644)
XLA Ops:
  0.0 65.9 %layer.1 = bf16[64,640]{1,0:T(8,128)(2,1)S(1)} custom-call(s32[1,1024]{1,0:T(1,128)} %bitcast.4, s32[1,1024]{1,0:T(1,128)} %bitcast.5, s32[2,16]{1,0:T(2,128)} %counts.1, bf16[128,5120]{1,0:T(8,128)(2,1)} %tokens.1, bf16[1,5120]{1,0:T(2,128)(2,1)} %bitcast.3, bf16[1,5120,512]{2,1,0:T(8,128)(2,1)} %w_gate.1, bf16[1,5120,512]{2,1,0:T(8,128)(2,1)} %w_up.1, ...), custom_call_target="tpu_custom_call" | custom-call | tf_op jit(solution)/shard_map/layer/pallas_call | solution.py:420
  65.9 0.6 copy.13

commit v7 on v6

--- a/solution.py
+++ b/solution.py
@@ -27,9 +27,9 @@
 def kernel(
     ids, mod, counts, tokens, router, w_gate, w_up, w_down, s_gate, s_up, s_down,
     out,
-    rows_in, wg, wu, wd, sg, su, sd0, sd1, xs, table, place,
+    rows_in, wg, wu, wd, sg, su, sd, xs, table, place,
     ysend0, ysend1, yrecv0, yrecv1, xsend0, xsend1, xrecv0, xrecv1, taken,
-    hid_e, eysend, eyrecv, exsend, exrecv, efar, egot, hilo, mine_h0, mine_h1, hid0, hid1, early, own, fsend, frecv,
+    hid_e, eysend, eyrecv, exsend, exrecv, efar, egot, hilo, mine_h0, mine_h1, hid0, hid1, own, fsend, frecv,
     load_sem, a_send, a_recv, s_send, s_recv, y_send, y_recv, x_send, x_recv, b_send, b_recv,
     ey_send, ey_recv, ex_send, ex_recv, ef_send, ef_recv, d_send, d_recv, w_send, w_recv, k_send, k_recv, f_send, f_recv,
 ):
@@ -38,10 +38,9 @@
     block, width = xs.shape[1], xs.shape[2]
     half = block // 2
     slots = table.shape[0]
-    sd, mine_h, hid = (sd0, sd1), (mine_h0, mine_h1), (hid0, hid1)
+    mine_h, hid = (mine_h0, mine_h1), (hid0, hid1)
     ysend, yrecv, xsend, xrecv = (ysend0, ysend1), (yrecv0, yrecv1), (xsend0, xsend1), (xrecv0, xrecv1)
-    sizes = (mine_h0.shape[1], mine_h1.shape[1])
-    spans = (slice(0, sizes[0]), slice(sizes[0], sizes[0] + sizes[1]))
+    quarter, hidden = half // 2, sg.shape[1]
     row = x * 2 + yl
     expert = yh * 8 + z * 2 + core
 
@@ -63,8 +62,11 @@
             src_ref=src, dst_ref=dst, send_sem=send, recv_sem=recv, device_id=device, device_id_type=MESH
         )
 
-    def units(q, of):
-        return pl.ds(pl.multiple_of(of * sizes[q], 128), sizes[q])
+    def units(of):
+        return pl.ds(pl.multiple_of(of * hidden, hidden), hidden)
+
+    def rows_of(of):
+        return pl.ds(pl.multiple_of(of * quarter, quarter), quarter)
 
     loads = [
         pltpu.make_async_copy(tokens, rows_in, load_sem.at[0]),
@@ -74,8 +76,7 @@
         pltpu.make_async_copy(w_gate.at[0], wg, load_sem.at[3]),
         pltpu.make_async_copy(w_up.at[0], wu, load_sem.at[4]),
         pltpu.make_async_copy(w_down.at[0], wd, load_sem.at[5]),
-        pltpu.make_async_copy(s_down.at[spans[0]], sd[0].at[units(0, core)], load_sem.at[6]),
-        pltpu.make_async_copy(s_down.at[spans[1]], sd[1].at[units(1, core)], load_sem.at[7]),
+        pltpu.make_async_copy(s_down, sd.at[units(core)], load_sem.at[6]),
     ]
     for load in loads:
         load.start()
@@ -136,12 +137,8 @@
             xsend[q].at[dx - 1], xrecv[q].at[dx - 1], x_send.at[q], x_recv.at[q, dx - 1], {"x": ahead(4 - dx)}
         )
 
-    w_out = [
-        remote(s_down.at[spans[q]], sd[q].at[units(q, core)], w_send.at[q], w_recv.at[q], sibling)
-        for q in (0, 1)
-    ]
-    for copy in w_out:
-        copy.start()
+    w_copy = remote(s_down, sd.at[units(core)], w_send, w_recv, sibling)
+    w_copy.start()
     ones = ones_of(expert)
     table[...] = ones.astype(BF16)
     place[:, : 2 * slots] = jnp.concatenate([ones, ones], axis=0).T.astype(BF16)
@@ -149,12 +146,14 @@
     place[:, 2 * slots :] = jnp.concatenate([ones, ones], axis=0).T.astype(BF16)
 
     def part(q, s):
-        return dot(xs[s], sg[:, spans[q]]), dot(xs[s], su[:, spans[q]])
+        low = q * quarter
+        rows = jnp.concatenate([xs[s, low : low + quarter], xs[s, half + low : half + low + quarter]], axis=0)
+        return dot(rows, sg[...]), dot(rows, su[...])
 
     def y_start(q, dx):
         gate, upper = part(q, dx * 2 + 1)
-        ysend[q][dx, :, : sizes[q]] = gate.astype(BF16)
-        ysend[q][dx, :, sizes[q] :] = upper.astype(BF16)
+        ysend[q][dx, :, :hidden] = gate.astype(BF16)
+        ysend[q][dx, :, hidden:] = upper.astype(BF16)
         y_copy(q, dx).start()
 
     for load in loads[1:4]:
@@ -196,12 +195,12 @@
     def pair_sum(q, dx):
         y_copy(q, dx).wait_recv()
         gate, upper = part(q, dx * 2)
-        return gate + yrecv[q][dx, :, : sizes[q]].astype(F32), upper + yrecv[q][dx, :, sizes[q] :].astype(F32)
+        return gate + yrecv[q][dx, :, :hidden].astype(F32), upper + yrecv[q][dx, :, hidden:].astype(F32)
 
     def pair_send(q, dx):
         gate, upper = pair_sum(q, dx)
-        xsend[q][dx - 1, :, : sizes[q]] = gate.astype(BF16)
-        xsend[q][dx - 1, :, sizes[q] :] = upper.astype(BF16)
+        xsend[q][dx - 1, :, :hidden] = gate.astype(BF16)
+        xsend[q][dx - 1, :, hidden:] = upper.astype(BF16)
         x_copy(q, dx).start()
 
     b_arrival(1).wait_recv()
@@ -237,13 +236,13 @@
     def d_copy(q, s, cross):
         target = to_row(s // 2, s % 2) | ({"core": 1 - core} if cross else {})
         return remote(
-            mine_h[q].at[his if cross else mine], hid[q].at[s, :, units(q, core)],
+            mine_h[q].at[rows_of(1 - core if cross else core)], hid[q].at[s, :, units(core)],
             d_send.at[q], d_recv.at[q, s, cross], target,
         )
 
     def d_arrival(q, s, cross):
-        there = units(q, 1 - core if cross else core)
-        return remote(mine_h[q].at[mine], hid[q].at[s, :, there], d_send.at[q], d_recv.at[q, s, cross], other_y)
+        there = units(1 - core if cross else core)
+        return remote(mine_h[q].at[rows_of(core)], hid[q].at[s, :, there], d_send.at[q], d_recv.at[q, s, cross], other_y)
 
     def d_relay(q, dx):
         s = dx * 2 + 1
@@ -253,10 +252,10 @@
         gate, upper = pair_sum(q, 0)
         for dx in (2, 1, 3):
             x_copy(q, dx).wait_recv()
-            gate = gate + xrecv[q][dx - 1, :, : sizes[q]].astype(F32)
-            upper = upper + xrecv[q][dx - 1, :, sizes[q] :].astype(F32)
+            gate = gate + xrecv[q][dx - 1, :, :hidden].astype(F32)
+            upper = upper + xrecv[q][dx - 1, :, hidden:].astype(F32)
         mine_h[q][...] = (silu(gate) * upper).astype(BF16)
-        hid[q][0, :, units(q, core)] = mine_h[q][mine, :]
+        hid[q][0, :, units(core)] = mine_h[q][rows_of(core), :]
         for s in (1, 2, 6, 0) if q == 0 else (1, 2, 6, 4, 0):
             for cross in (0, 1):
                 if s or cross:
@@ -271,7 +270,7 @@
             copy.start()
 
     def d_onward(q, dx):
-        rows = pl.ds(0 if dx == 1 else half // 2, half // 2)
+        rows = pl.ds(0 if dx == 1 else quarter // 2, quarter // 2)
         return remote(
             hid[q].at[dx * 2, rows], hid[q].at[4, rows], d_send.at[q], d_recv.at[q, 4, dx // 2], {"x": ahead(dx)}
         )
@@ -327,65 +326,67 @@
     hilo[slots : 2 * slots] = (total - high.astype(F32)).astype(BF16)
     k_copy = remote(hilo.at[: 2 * slots], hilo.at[2 * slots :], k_send, k_recv, sibling)
     k_copy.start()
+    loads[7].wait()
+    w_copy.wait_recv()
     for q in (0, 1):
-        loads[7 + q].wait()
-        w_out[q].wait_recv()
         d_arrival(q, 0, 1).wait_recv()
 
-    def f_copy(s, q):
-        target = {"yh": lax.rem(yh + q // 4, 2), "z": lax.rem(z + q % 4, 4)}
-        return remote(fsend.at[s], frecv.at[q - 1], f_send, f_recv.at[q - 1], target)
-
-    def begin(s):
-        tokens_of = pl.ds(pl.multiple_of(owner(s) * block + core * half, half), half)
-        return dot(hid[0][s], sd[0][...]) + dot(place[tokens_of, :], hilo[...])
-
-    def finish(s, begun=None):
+    def f_copy(q, s, to):
+        target = {"yh": lax.rem(yh + to // 4, 2), "z": lax.rem(z + to % 4, 4)}
+        return remote(fsend.at[q, s], frecv.at[q, to - 1], f_send.at[q], f_recv.at[q, to - 1], target)
+
+    def finish(s, chunks):
         j = owner(s)
-        total = (begin(s) if begun is None else begun) + dot(hid[1][s], sd[1][...])
-        q = lax.rem(j // 4 + yh, 2) * 4 + lax.rem(lax.rem(j, 4) + 4 - z, 4)
-
-        @pl.when(q == 0)
+        count = quarter * len(chunks)
+        tokens_of = pl.ds(pl.multiple_of(j * block + core * half + chunks[0] * quarter, quarter), count)
+        units_of = hid[chunks[0]][s] if len(chunks) == 1 else jnp.concatenate([hid0[s], hid1[s]], axis=0)
+        total = dot(units_of, sd[...]) + dot(place[tokens_of, :], hilo[...])
+        to = lax.rem(j // 4 + yh, 2) * 4 + lax.rem(lax.rem(j, 4) + 4 - z, 4)
+
+        @pl.when(to == 0)
         def _():
-            own[...] = total
-
-        @pl.when(q > 0)
+            for i, q in enumerate(chunks):
+                own[q] = total[i * quarter : (i + 1) * quarter]
+
+        @pl.when(to > 0)
         def _():
-            fsend[s] = total.astype(BF16)
-            f_copy(s, q).start()
+            for i, q in enumerate(chunks):
+                fsend[q, s] = total[i * quarter : (i + 1) * quarter].astype(BF16)
+                f_copy(q, s, to).start()
 
     for dx in (1, 3):
         block_across(0, dx)
     block_relay(1, (1, 3, 2))
     k_copy.wait_recv()
-    finish(0)
-    finish(1)
+    finish(0, (0, 1))
+    finish(1, (0, 1))
+
     def end_direct(s):
         d_arrival(1, s, 0).wait_recv()
         d_arrival(1, s, 1).wait_recv()
-        finish(s)
-
-    def begin_far(dx):
-        d_relay(0, dx).wait_recv()
-        early[dx - 1] = begin(dx * 2 + 1)
+        finish(s, (0, 1))
+
+    def end_far(q, dx):
+        d_relay(q, dx).wait_recv()
+        finish(dx * 2 + 1, (q,))
 
     end_direct(2)
     end_direct(6)
-    begin_far(1)
-    begin_far(3)
+    end_far(0, 1)
+    end_far(0, 3)
     d_onward(0, 1).wait_recv()
     d_onward(0, 3).wait_recv()
     end_direct(4)
-    begin_far(2)
+    end_far(0, 2)
     for dx in (1, 3, 2):
-        d_relay(1, dx).wait_recv()
-        finish(dx * 2 + 1, early[dx - 1])
-
-    total = own[...]
-    for q in range(1, ROWS):
-        f_copy(0, q).wait_recv()
-        total = total + frecv[q - 1].astype(F32)
-    out[...] = total.astype(BF16)
+        end_far(1, dx)
+
+    for q in (0, 1):
+        total = own[q]
+        for to in range(1, ROWS):
+            f_copy(q, 0, to).wait_recv()
+            total = total + frecv[q, to - 1].astype(F32)
+        out[q * quarter : (q + 1) * quarter, :] = total.astype(BF16)
 
     def left(bytes_of, sem):
         pltpu.make_async_copy(bytes_of, bytes_of, sem).wait()
@@ -396,13 +397,13 @@
     for q in (0, 1):
         left(ysend[q], y_send.at[q])
         left(xsend[q], x_send.at[q])
-        left(xs.at[:3, :, : 5 * sizes[q] // 2], d_send.at[q])
-        w_out[q].wait_send()
+        left(xs.at[:3], d_send.at[q])
+        left(frecv.at[q], f_send.at[q])
     left(eysend.at[:3], ey_send)
     left(eysend.at[:2], ex_send)
     far_copy.wait_send()
     k_copy.wait_send()
-    left(frecv, f_send)
+    w_copy.wait_send()
 
 
 def per_device(tokens, expert_ids, modality, tile_counts, router, w_gate, w_up, w_down, shared_gate, shared_up, shared_down):
@@ -412,7 +413,7 @@
     inner = w_gate.shape[2]
     slots = 2 * MAXT * TILE
     half = block // 2
-    sizes = (256, hidden - 256)
+    quarter = half // 2
     count = expert_ids.shape[0]
     vmem = pl.BlockSpec(memory_space=pltpu.VMEM)
     hbm = pl.BlockSpec(memory_space=pl.ANY)
@@ -430,12 +431,12 @@
             pltpu.VMEM((inner, depth), BF16),
             pltpu.VMEM((width, hidden), BF16),
             pltpu.VMEM((width, hidden), BF16),
-            *(pltpu.VMEM((2 * size, width), BF16) for size in sizes),
+            pltpu.VMEM((2 * hidden, width), BF16),
             pltpu.VMEM((ROWS, block, width), BF16),
             pltpu.VMEM((slots, count), BF16),
             pltpu.VMEM((count, 4 * slots), BF16),
-            *(pltpu.VMEM((4, block, 2 * size), BF16) for size in sizes + sizes),
-            *(pltpu.VMEM((3, block, 2 * size), BF16) for size in sizes + sizes),
+            *[pltpu.VMEM((4, half, 2 * hidden), BF16)] * 4,
+            *[pltpu.VMEM((3, half, 2 * hidden), BF16)] * 4,
             pltpu.VMEM((ROWS, slots, width), BF16),
             pltpu.VMEM((slots, inner), BF16),
             pltpu.VMEM((4, slots, width), BF16),
@@ -445,18 +446,17 @@
             pltpu.VMEM((2, slots, width), BF16),
             pltpu.VMEM((2, slots, width), BF16),
             pltpu.VMEM((4 * slots, width), BF16),
-            *(pltpu.VMEM((block, size), BF16) for size in sizes),
-            *(pltpu.VMEM((ROWS, half, 2 * size), BF16) for size in sizes),
-            pltpu.VMEM((3, half, width), F32),
-            pltpu.VMEM((half, width), F32),
-            pltpu.VMEM((ROWS, half, width), BF16),
-            pltpu.VMEM((ROWS - 1, half, width), BF16),
+            *[pltpu.VMEM((half, hidden), BF16)] * 2,
+            *[pltpu.VMEM((ROWS, quarter, 2 * hidden), BF16)] * 2,
+            pltpu.VMEM((2, quarter, width), F32),
+            pltpu.VMEM((2, ROWS, quarter, width), BF16),
+            pltpu.VMEM((2, ROWS - 1, quarter, width), BF16),
             dma((10,)),
             dma, dma((ROWS,)), dma, dma((ROWS,)),
             dma((2,)), dma((2, 4)), dma((2,)), dma((2, 3)),
             dma, dma((ROWS,)),
             dma, dma((4,)), dma, dma((4,)), dma, dma,
-            dma((2,)), dma((2, ROWS, 2)), dma((2,)), dma((2,)), dma, dma, dma, dma((ROWS - 1,)),
+            dma((2,)), dma((2, ROWS, 2)), dma, dma, dma, dma, dma((2,)), dma((2, ROWS - 1)),
         ],
         compiler_params=pltpu.CompilerParams(
             collective_id=0, has_side_effects=True, vmem_limit_bytes=60 * 1024 * 1024

time: 66.7 us -> 65.4 us (0.981)
  Pallas kernels: 65.9 us -> 64.6 us
    pallas_call x1, Pallas kernels: 65.9 us -> 64.6 us  [per_device(): pl.pallas_call(kernel, name='layer', out_shape=pltpu.VMEM((half, width),...]
where the time goes in v7:
time: 65.4 us; the launch traced here: 65.3 us
  Pallas kernels  64.6 us (99%)
    pallas_call x1, Pallas kernels, per_device(): pl.pallas_call(kernel, name='layer', out_shape=pltpu.VMEM((half, width),...  64.6 us

profile of v7, /device:TPU:25, one launch (start us, length us, event | category | flops | bytes accessed | tf_op | source)
XLA Modules:
  0.0 65.3 jit_solution(2309261021375894838)
XLA Ops:
  0.0 64.6 %layer.1 = bf16[64,640]{1,0:T(8,128)(2,1)S(1)} custom-call(s32[1,1024]{1,0:T(1,128)} %bitcast.4, s32[1,1024]{1,0:T(1,128)} %bitcast.5, s32[2,16]{1,0:T(2,128)} %counts.1, bf16[128,5120]{1,0:T(8,128)(2,1)} %tokens.1, bf16[1,5120]{1,0:T(2,128)(2,1)} %bitcast.3, bf16[1,5120,512]{2,1,0:T(8,128)(2,1)} %w_gate.1, bf16[1,5120,512]{2,1,0:T(8,128)(2,1)} %w_up.1, ...), custom_call_target="tpu_custom_call" | custom-call | tf_op jit(solution)/shard_map/layer/pallas_call | solution.py:421
  64.6 0.6 copy.13

commit v8 on v7

--- a/solution.py
+++ b/solution.py
@@ -115,14 +115,14 @@
         target = ahead(dx) * 2 + lax.rem(yl + dy, 2)
         return remote(
             rows_in.at[mine, pl.ds(pl.multiple_of(target * width, 128), width)],
-            xs.at[s, mine], a_send, a_recv.at[s], to_row(dx, dy),
+            xs.at[s, mine], a_send, a_recv.at[s - 1], to_row(dx, dy),
         )
 
     def s_copy(s):
-        return remote(xs.at[s, mine], xs.at[s, mine], s_send, s_recv.at[s], sibling)
+        return remote(xs.at[s, mine], xs.at[s, mine], s_send, s_recv.at[s - 1], sibling)
 
     def s_arrival(s):
-        return remote(xs.at[s, his], xs.at[s, his], s_send, s_recv.at[s], sibling)
+        return remote(xs.at[s, his], xs.at[s, his], s_send, s_recv.at[s - 1], sibling)
 
     order = (5, 3, 7, 1, 4, 2, 6)
     loads[0].wait()
@@ -180,10 +180,7 @@
 
     def b_copy(source, dx, dy):
         s = dx * 2 + dy if source == 0 else dx * 2 + 1
-        return remote(taken.at[source], taken.at[s], b_send, b_recv.at[s], to_row(dx, dy))
-
-    def b_arrival(s):
-        return remote(taken.at[s], taken.at[s], b_send, b_recv.at[s], other_y)
+        return remote(taken.at[source], taken.at[s], b_send, b_recv.at[0 if s == 1 else 1], to_row(dx, dy))
 
     b_out = [b_copy(0, 0, 1), b_copy(0, 2, 0), b_copy(0, 1, 0), b_copy(0, 3, 0)]
     for copy in b_out:
@@ -203,7 +200,7 @@
         xsend[q][dx - 1, :, hidden:] = upper.astype(BF16)
         x_copy(q, dx).start()
 
-    b_arrival(1).wait_recv()
+    b_out[0].wait_recv()
     relayed = [b_copy(1, dx, 0) for dx in (2, 1, 3)]
     for copy in relayed:
         copy.start()
@@ -211,8 +208,7 @@
     for dx in (2, 1, 3):
         pair_send(0, dx)
 
-    for s in (2, 3, 4, 5, 6, 7):
-        b_arrival(s).wait_recv()
+    pltpu.make_async_copy(taken.at[2:], taken.at[2:], b_recv.at[1]).wait()
     loads[4].wait()
     loads[5].wait()
 
@@ -233,20 +229,25 @@
     gate, upper = lax.fori_loop(0, ROWS, expert_part, (zero, zero))
     hid_e[...] = (silu(gate) * upper).astype(BF16)
 
+    ARRIVALS = ((0, 1), (1, 0), (1, 1), (2, 0), (2, 1), (3, 0), (4, 0), (4, 1), (5, 0), (6, 0), (6, 1), (7, 0))
+
+    def d_sem(q, s, cross):
+        return d_recv.at[q, ARRIVALS.index((s, cross))]
+
     def d_copy(q, s, cross):
         target = to_row(s // 2, s % 2) | ({"core": 1 - core} if cross else {})
         return remote(
             mine_h[q].at[rows_of(1 - core if cross else core)], hid[q].at[s, :, units(core)],
-            d_send.at[q], d_recv.at[q, s, cross], target,
+            d_send.at[q], d_sem(q, s, cross), target,
         )
 
     def d_arrival(q, s, cross):
         there = units(1 - core if cross else core)
-        return remote(mine_h[q].at[rows_of(core)], hid[q].at[s, :, there], d_send.at[q], d_recv.at[q, s, cross], other_y)
+        return remote(mine_h[q].at[rows_of(core)], hid[q].at[s, :, there], d_send.at[q], d_sem(q, s, cross), other_y)
 
     def d_relay(q, dx):
         s = dx * 2 + 1
-        return remote(hid[q].at[1], hid[q].at[s], d_send.at[q], d_recv.at[q, s, 0], to_row(dx, 0))
+        return remote(hid[q].at[1], hid[q].at[s], d_send.at[q], d_sem(q, s, 0), to_row(dx, 0))
 
     def block_end(q):
         gate, upper = pair_sum(q, 0)
@@ -272,7 +273,7 @@
     def d_onward(q, dx):
         rows = pl.ds(0 if dx == 1 else quarter // 2, quarter // 2)
         return remote(
-            hid[q].at[dx * 2, rows], hid[q].at[4, rows], d_send.at[q], d_recv.at[q, 4, dx // 2], {"x": ahead(dx)}
+            hid[q].at[dx * 2, rows], hid[q].at[4, rows], d_send.at[q], d_sem(q, 4, dx // 2), {"x": ahead(dx)}
         )
 
     def block_across(q, dx):
@@ -280,7 +281,7 @@
         for cross in (0, 1):
             d_arrival(q, s, cross).wait_recv()
         d_onward(q, dx).start()
-        copy = remote(hid[q].at[s], hid[q].at[s + 1], d_send.at[q], d_recv.at[q, s + 1, 0], other_y)
+        copy = remote(hid[q].at[s], hid[q].at[s + 1], d_send.at[q], d_sem(q, s + 1, 0), other_y)
         copy.start()
 
     def result_part(dx, dy):
@@ -288,10 +289,10 @@
         return dot(hid_e[...], wd[:, pl.ds(pl.multiple_of(target * width, 128), width)])
 
     def ey_copy(dx):
-        return remote(eysend.at[dx], eyrecv.at[dx], ey_send, ey_recv.at[dx], other_y)
+        return remote(eysend.at[dx], eyrecv.at[dx], ey_send, ey_recv.at[(dx + 1) // 2], other_y)
 
     def ex_copy(dx):
-        return remote(exsend.at[dx], exrecv.at[dx], ex_send, ex_recv.at[dx], {"x": ahead(4 - dx)})
+        return remote(exsend.at[dx], exrecv.at[dx], ex_send, ex_recv.at[dx // 2], {"x": ahead(4 - dx)})
 
     far_copy = remote(efar, egot, ef_send, ef_recv, {"x": ahead(2)})
 
@@ -452,11 +453,11 @@
             pltpu.VMEM((2, ROWS, quarter, width), BF16),
             pltpu.VMEM((2, ROWS - 1, quarter, width), BF16),
             dma((10,)),
-            dma, dma((ROWS,)), dma, dma((ROWS,)),
+            dma, dma((ROWS - 1,)), dma, dma((ROWS - 1,)),
             dma((2,)), dma((2, 4)), dma((2,)), dma((2, 3)),
-            dma, dma((ROWS,)),
-            dma, dma((4,)), dma, dma((4,)), dma, dma,
-            dma((2,)), dma((2, ROWS, 2)), dma, dma, dma, dma, dma((2,)), dma((2, ROWS - 1)),
+            dma, dma((2,)),
+            dma, dma((3,)), dma, dma((2,)), dma, dma,
+            dma((2,)), dma((2, 12)), dma, dma, dma, dma, dma((2,)), dma((2, ROWS - 1)),
         ],
         compiler_params=pltpu.CompilerParams(
             collective_id=0, has_side_effects=True, vmem_limit_bytes=60 * 1024 * 1024

time: 65.4 us -> 65.3 us (level)
  no operation moved by 1% of the time
where the time goes in v8:
time: 65.3 us; the launch traced here: 65.1 us
  Pallas kernels  64.4 us (99%)
    pallas_call x1, Pallas kernels, per_device(): pl.pallas_call(kernel, name='layer', out_shape=pltpu.VMEM((half, width),...  64.4 us

profile of v8, /device:TPU:25, one launch (start us, length us, event | category | flops | bytes accessed | tf_op | source)
XLA Modules:
  0.0 65.1 jit_solution(9690186215955213782)
XLA Ops:
  0.0 64.4 %layer.1 = bf16[64,640]{1,0:T(8,128)(2,1)S(1)} custom-call(s32[1,1024]{1,0:T(1,128)} %bitcast.4, s32[1,1024]{1,0:T(1,128)} %bitcast.5, s32[2,16]{1,0:T(2,128)} %counts.1, bf16[128,5120]{1,0:T(8,128)(2,1)} %tokens.1, bf16[1,5120]{1,0:T(2,128)(2,1)} %bitcast.3, bf16[1,5120,512]{2,1,0:T(8,128)(2,1)} %w_gate.1, bf16[1,5120,512]{2,1,0:T(8,128)(2,1)} %w_up.1, ...), custom_call_target="tpu_custom_call" | custom-call | tf_op jit(solution)/shard_map/layer/pallas_call | solution.py:422
  64.5 0.6 copy.13
